TPU v7x, 32 devices: a 4x4x1 block of a 4x4x8 slice. The times are simulated.
32 devices in a mesh: dp: 1 (over z), tp: 32 (over y, x, core).
Axes of the slice: x: 4, y: 4, z: 1, core: 2. Of those that a mesh axis runs over, the one named last changes fastest.
The devices are a block of a 4x4x8 slice.
Arguments:
- act_in: bfloat16 [512, 4096], P('dp')
- w_qkv: bfloat16 [3, 4096, 32, 3, 128], P(None, None, 'tp')
- w_out: bfloat16 [3, 32, 128, 4096], P(None, 'tp')
- w_up: bfloat16 [3, 4096, 16384], P(None, None, 'tp')
- w_down: bfloat16 [3, 16384, 4096], P(None, 'tp')
- gain_one: float32 [3, 4096], replicated
- gain_two: float32 [3, 4096], replicated
Outputs:
- output: bfloat16 [512, 4096], P('dp')
All inputs are finite; a program needn't handle non-finite values.
Results may differ from a plain program's by a relative error of at most 0.02.
Values are sent between devices in bfloat16 or wider.
A program may use at most 768 MiB of HBM per device.

v0:
```python
import math
import jax
import jax.numpy as jnp
from jax import lax
from jax.sharding import PartitionSpec as P


def layer_norm(act_rows, gain_vec):
    rows_f32 = act_rows.astype(jnp.float32)
    centred = rows_f32 - jnp.mean(rows_f32, axis=-1, keepdims=True)
    var_rows = jnp.mean(centred * centred, axis=-1, keepdims=True)
    return (centred * lax.rsqrt(var_rows + 1e-5) * gain_vec).astype(jnp.bfloat16)


def causal_attention(query_rows, key_rows, value_rows, query_start):
    n_q, num_heads, head_dim = query_rows.shape
    seq_k = key_rows.shape[0]
    limit_rows = max(8, 2 ** 24 // (num_heads * seq_k))
    row_block = math.gcd(n_q, 2 ** int(math.log2(limit_rows)))
    score_scale = 1.0 / math.sqrt(head_dim)
    key_pos = jnp.arange(seq_k)

    def one_block(blk_idx):
        row_start = blk_idx * row_block
        q_blk = lax.dynamic_slice_in_dim(query_rows, row_start, row_block, axis=0)
        scores = jnp.einsum("qhd,khd->hqk", q_blk, key_rows, preferred_element_type=jnp.float32) * score_scale
        q_pos = query_start + row_start + jnp.arange(row_block)
        scores = jnp.where(key_pos[None, None, :] <= q_pos[None, :, None], scores, -1e30)
        exp_scores = jnp.exp(scores - jnp.max(scores, axis=-1, keepdims=True))
        prob_sum = jnp.sum(exp_scores, axis=-1)
        mix_out = jnp.einsum("hqk,khd->qhd", exp_scores.astype(jnp.bfloat16), value_rows, preferred_element_type=jnp.float32)
        return (mix_out / prob_sum.T[:, :, None]).astype(jnp.bfloat16)

    blocks = lax.map(one_block, jnp.arange(n_q // row_block))
    return blocks.reshape(n_q, num_heads, head_dim)


def solution(mesh):
    def device_fn(act_in, w_qkv, w_out, w_up, w_down, gain_one, gain_two):
        act_rows = act_in
        for layer_idx in range(w_qkv.shape[0]):
            normed = layer_norm(act_rows, gain_one[layer_idx])
            qkv_rows = jnp.einsum("sm,mhcd->shcd", normed, w_qkv[layer_idx], preferred_element_type=jnp.float32).astype(jnp.bfloat16)
            attn_rows = causal_attention(qkv_rows[:, :, 0], qkv_rows[:, :, 1], qkv_rows[:, :, 2], 0)
            part_sum = jnp.einsum("shd,hdm->sm", attn_rows, w_out[layer_idx], preferred_element_type=jnp.float32).astype(jnp.bfloat16)
            attn_sum = lax.psum(part_sum, "tp")
            act_rows = (act_rows.astype(jnp.float32) + attn_sum.astype(jnp.float32)).astype(jnp.bfloat16)
            normed = layer_norm(act_rows, gain_two[layer_idx])
            hidden = jax.nn.gelu(jnp.dot(normed, w_up[layer_idx], preferred_element_type=jnp.float32), approximate=True).astype(jnp.bfloat16)
            part_sum = jnp.dot(hidden, w_down[layer_idx], preferred_element_type=jnp.float32).astype(jnp.bfloat16)
            mlp_sum = lax.psum(part_sum, "tp")
            act_rows = (act_rows.astype(jnp.float32) + mlp_sum.astype(jnp.float32)).astype(jnp.bfloat16)
        return act_rows

    return jax.shard_map(
        device_fn,
        mesh=mesh,
        in_specs=(
            P("dp", None),
            P(None, None, "tp", None, None),
            P(None, "tp", None, None),
            P(None, None, "tp"),
            P(None, "tp", None),
            P(None, None),
            P(None, None),
        ),
        out_specs=P("dp", None),
        check_vma=False,
    )
```

profile of v0, /device:TPU:97, one launch (start us, length us, event | category | flops | bytes accessed | tf_op | source)
XLA Modules:
  0.0 733.7 jit_solution(3665425418107593633)
XLA Ops:
  6.5 0.0 copy-start.6
  6.5 0.0 all-reduce.7.cloned.1.call-start
  6.6 3.0 convert_reduce_fusion.5
  9.5 3.4 fusion.27
  13.0 0.0 copy-done.6
  13.0 0.0 copy-done.1
  13.0 4.3 fusion.106
  17.3 0.0 copy-start.7
  17.3 0.3 fusion.202
  17.6 0.2 fusion.174
  17.8 4.8 convolution_convert_fusion.2
  22.6 0.1 all-reduce.7.cloned.1.call-update
  22.7 0.4 all-reduce.9.cloned.1.call-start
  23.1 0.0 copy-done.7
  23.1 104.9 %all-reduce.7.cloned.1.call-done = bf16[512,4096]{1,0:T(8,128)(2,1)} async-done(((bf16[512,4096]{1,0:T(8,128)(2,1)}), bf16[512,4096]{1,0:T(8,128)(2,1)}) %all-reduce.7.cloned.1.call-update) | async-done | bytes 4194320 | tf_op jit(solution)/shard_map/psum | solution.py:46
  128.0 5.2 convert_reduce_fusion.4
  133.2 0.0 copy-start.5
  133.2 1.2 fusion.24
  134.4 5.0 fusion.131
  139.4 0.0 copy-done.5
  139.5 6.6 convolution_convert_fusion.5
  146.1 0.1 all-reduce.9.cloned.1.call-update
  146.1 0.6 all-reduce.11.cloned.1.call-start
  146.7 100.3 %all-reduce.9.cloned.1.call-done = bf16[512,4096]{1,0:T(8,128)(2,1)} async-done(((bf16[512,4096]{1,0:T(8,128)(2,1)}), bf16[512,4096]{1,0:T(8,128)(2,1)}) %all-reduce.9.cloned.1.call-update) | async-done | bytes 4194320 | tf_op jit(solution)/shard_map/psum | solution.py:51
  247.0 5.2 convert_reduce_fusion.3
  252.2 0.0 copy-start.3
  252.2 1.2 fusion.21
  253.4 4.5 fusion.101
  257.9 0.0 copy-done.3
  257.9 0.3 fusion.203
  258.2 0.2 fusion.176
  258.4 4.8 convolution_convert_fusion.1
  263.3 0.1 all-reduce.11.cloned.1.call-update
  263.3 0.2 all-reduce.13.cloned.1.call-start
  263.6 100.6 %all-reduce.11.cloned.1.call-done = bf16[512,4096]{1,0:T(8,128)(2,1)} async-done(((bf16[512,4096]{1,0:T(8,128)(2,1)}), bf16[512,4096]{1,0:T(8,128)(2,1)}) %all-reduce.11.cloned.1.call-update) | async-done | bytes 4194320 | tf_op jit(solution)/shard_map/psum | solution.py:46
  364.2 5.2 convert_reduce_fusion.2
  369.3 0.0 copy-start.4
  369.3 1.2 fusion.18
  370.6 5.0 fusion.147
  375.6 0.0 copy-done.4
  375.6 6.6 convolution_convert_fusion.4
  382.2 0.1 all-reduce.13.cloned.1.call-update
  382.3 0.3 all-reduce.15.cloned.1.call-start
  382.6 100.6 %all-reduce.13.cloned.1.call-done = bf16[512,4096]{1,0:T(8,128)(2,1)} async-done(((bf16[512,4096]{1,0:T(8,128)(2,1)}), bf16[512,4096]{1,0:T(8,128)(2,1)}) %all-reduce.13.cloned.1.call-update) | async-done | bytes 4194320 | tf_op jit(solution)/shard_map/psum | solution.py:51
  483.1 5.2 convert_reduce_fusion.1
  488.3 0.0 copy-start.2
  488.3 1.2 fusion.15
  489.6 4.5 fusion.96
  494.0 0.0 copy-done.2
  494.1 0.3 fusion.204
  494.4 0.2 fusion.178
  494.6 4.8 convolution_convert_fusion
  499.4 0.1 all-reduce.15.cloned.1.call-update
  499.4 0.3 all-reduce.17.cloned.1.call-start
  499.8 100.5 %all-reduce.15.cloned.1.call-done = bf16[512,4096]{1,0:T(8,128)(2,1)} async-done(((bf16[512,4096]{1,0:T(8,128)(2,1)}), bf16[512,4096]{1,0:T(8,128)(2,1)}) %all-reduce.15.cloned.1.call-update) | async-done | bytes 4194320 | tf_op jit(solution)/shard_map/psum | solution.py:46
  600.3 5.2 convert_reduce_fusion
  605.5 0.0 copy-start
  605.5 1.2 fusion.12
  606.7 5.0 fusion.163
  611.8 0.0 copy-done
  611.8 6.6 convolution_convert_fusion.3
  618.4 0.1 all-reduce.17.cloned.1.call-update
  618.4 100.9 %all-reduce.17.cloned.1.call-done = bf16[512,4096]{1,0:T(8,128)(2,1)} async-done(((bf16[512,4096]{1,0:T(8,128)(2,1)}), bf16[512,4096]{1,0:T(8,128)(2,1)}) %all-reduce.17.cloned.1.call-update) | async-done | bytes 4194320 | tf_op jit(solution)/shard_map/psum | solution.py:51
  719.3 7.2 fusion.35
  (15 shorter events, 0.1 us)
Async XLA Ops:
  6.5 6.4 copy-start.6
  6.5 121.5 %all-reduce.7.cloned.1.call-start = ((), (), s32[]{:S(2)}) async-start(), calls=%async_computation | async-start | bytes 8388608 | tf_op jit(solution)/shard_map/psum | solution.py:46
  6.6 6.5 copy-start.1
  17.3 5.8 copy-start.7
  22.7 224.3 %all-reduce.9.cloned.1.call-start = ((), (), s32[]{:S(2)}) async-start(), calls=%async_computation.1 | async-start | bytes 8388608 | tf_op jit(solution)/shard_map/psum | solution.py:51
  133.2 6.3 copy-start.5
  146.1 218.0 %all-reduce.11.cloned.1.call-start = ((), (), s32[]{:S(2)}) async-start(), calls=%async_computation.2 | async-start | bytes 8388608 | tf_op jit(solution)/shard_map/psum | solution.py:46
  252.2 5.7 copy-start.3
  263.3 219.8 %all-reduce.13.cloned.1.call-start = ((), (), s32[]{:S(2)}) async-start(), calls=%async_computation.3 | async-start | bytes 8388608 | tf_op jit(solution)/shard_map/psum | solution.py:51
  369.3 6.3 copy-start.4
  382.3 218.0 %all-reduce.15.cloned.1.call-start = ((), (), s32[]{:S(2)}) async-start(), calls=%async_computation.4 | async-start | bytes 8388608 | tf_op jit(solution)/shard_map/psum | solution.py:46
  488.3 5.7 copy-start.2
  499.4 219.9 %all-reduce.17.cloned.1.call-start = ((), (), s32[]{:S(2)}) async-start(), calls=%async_computation.5 | async-start | bytes 8388608 | tf_op jit(solution)/shard_map/psum | solution.py:51
  605.5 6.3 copy-start
Sparse Core Ops, SparseCore 0:
  22.8 105.1 all-reduce.6
  146.3 100.6 all-reduce.8
  263.4 100.6 all-reduce.10
  382.4 100.6 all-reduce.12
  499.6 100.7 all-reduce.14
  618.5 100.7 all-reduce.16
where the time goes:
time: 739 us; the launch traced here: 734 us
  waiting for transfers between devices  608 us (82%)
  matrix products  63.4 us (9%)
  other arithmetic  46.3 us (6%)
  between operations  14 us (2%)
    psum x3, waiting for transfers between devices, device_fn(): attn_sum = lax.psum(part_sum, 'tp')  306 us
    psum x3, waiting for transfers between devices, device_fn(): mlp_sum = lax.psum(part_sum, 'tp')  302 us
    reduce_sum x6, other arithmetic, layer_norm(): centred = rows_f32 - jnp.mean(rows_f32, axis=-1, keepdims=True)  28.8 us
    dot_general x3, matrix products, device_fn(): jnp.dot(hidden, w_down[layer_idx], preferred_element_type=jnp.float32)  19.8 us
    dot_general x3, matrix products, device_fn(): jnp.dot(normed, w_up[layer_idx], preferred_element_type=jnp.float32)  15 us
  transfers between devices with their start and end apart: 6, of which 6 were waited for; matrix products, arithmetic and copies ran while one was open for 0% of the time, Pallas kernels for 0%

commit v1 on v0

v1 whole, which is shorter than its diff:
```python
import functools
import math
import jax
import jax.numpy as jnp
from jax import lax
from jax.experimental import pallas as pl
from jax.experimental.pallas import tpu as pltpu
from jax.sharding import PartitionSpec as P

F32 = jnp.float32
BF16 = jnp.bfloat16
SIDE = 4
CORES = 2
TILES = 8


def norm_rows(rows, gain):
    centred = rows - jnp.mean(rows, axis=-1, keepdims=True)
    var = jnp.mean(centred * centred, axis=-1, keepdims=True)
    return centred * lax.rsqrt(var + 1e-5) * gain


def stack_kernel(act, hq, ho, hu, hd, gains, out,
                 wq, wo, wu, wd, part, psnd, prcv, tb, db, eb, tb2, db2, eb2,
                 kc, vc, ob, hid, xres,
                 wsem, pss, psr, rss, rsr, ags, agr, dds, ddr):
    layers = hq.shape[0]
    rows = act.shape[1] * act.shape[2] * act.shape[3]
    brow = act.shape[3]
    width = act.shape[4]
    head = hq.shape[3]
    tile = width // TILES
    halves = 2 * layers
    slots = CORES * halves
    scale = 1.0 / math.sqrt(head)

    t = lax.axis_index("tp")
    z = lax.axis_index("dp")
    m = lax.rem(t, CORES)
    x = lax.rem(lax.div(t, CORES), SIDE)
    y = lax.div(t, CORES * SIDE)
    partner = t + 1 - 2 * m

    def dev(yy, xx):
        return (yy * SIDE + xx) * CORES + m

    def ring(along_x):
        me = x if along_x else y
        r, o, l = (lax.rem(me + k, SIDE) for k in (1, 2, 3))
        if along_x:
            return me, r, l, o, dev(y, r), dev(y, l)
        return me, r, l, o, dev(r, x), dev(l, x)

    rings = {True: ring(True), False: ring(False)}

    barrier = pltpu.get_barrier_semaphore()
    peers = [partner, rings[True][4], rings[True][5], rings[False][4], rings[False][5]]
    for peer in peers:
        pl.semaphore_signal(barrier, inc=1, device_id=(z, peer), device_id_type=pl.DeviceIdType.MESH)

    def weight_copies(l, kind):
        if kind == 0:
            cps = [pltpu.make_async_copy(
                hq.at[l, c], wq.at[l, :, pl.ds(c * head, head)], wsem.at[l, c]) for c in range(3)]
            return cps + [pltpu.make_async_copy(ho.at[l], wo.at[l], wsem.at[l, 3])]
        return [pltpu.make_async_copy(hu.at[l], wu.at[l], wsem.at[l, 4]),
                pltpu.make_async_copy(hd.at[l], wd.at[l], wsem.at[l, 5])]

    for l in range(layers):
        for kind in range(2):
            for cp in weight_copies(l, kind):
                cp.start()

    kc[...] = jnp.zeros_like(kc)
    vc[...] = jnp.zeros_like(vc)

    def first_norm(i, carry):
        c = lax.div(i, SIDE)
        b = lax.rem(i, SIDE)
        out[c, b] = norm_rows(act[c, b].astype(F32), gains[0]).astype(BF16)
        return carry

    lax.fori_loop(0, CORES * SIDE, first_norm, 0)
    xres[...] = act[m, y, x]

    pl.semaphore_wait(barrier, len(peers))

    def remote(src, dst, ss, rs, peer):
        return pltpu.make_async_remote_copy(
            src_ref=src, dst_ref=dst, send_sem=ss, recv_sem=rs,
            device_id=(z, peer), device_id_type=pl.DeviceIdType.MESH)

    quarter = width // 4

    def cols(o):
        h1 = pl.ds(2 * o * quarter, quarter)
        h2 = pl.ds((2 * o + 1) * quarter, quarter)
        return h1, h2, pl.ds(2 * o * quarter, 2 * quarter)

    def rs_blk(o, ph, b, cs):
        if ph == 0:
            return part.at[:, b, :, cs] if o == 0 else part.at[b, :, :, cs]
        return part.at[b, x, :, cs] if o == 0 else part.at[y, b, :, cs]

    def rs_desc(o, ph, k):
        me, r, l, op, rdev, ldev = rings[(o + ph) % 2 == 0]
        h1, h2, _ = cols(o)
        tt, dd, ee = (tb, db, eb) if ph == 0 else (tb2, db2, eb2)
        b, cs, dst, to = [
            (op, h1, tt.at[o, 0], rdev), (op, h2, tt.at[o, 1], ldev),
            (r, h2, dd.at[o, 0], rdev), (l, h1, dd.at[o, 1], ldev),
            (r, h1, ee.at[o, 0], rdev), (l, h2, ee.at[o, 1], ldev)][k]
        return remote(rs_blk(o, ph, b, cs), dst, rss.at[o, ph, k], rsr.at[o, ph, k], to)

    def rs_start(o, ph):
        for k in range(4):
            rs_desc(o, ph, k).start()

    def rs_fwd(o, ph):
        _, r, l, _, _, _ = rings[(o + ph) % 2 == 0]
        h1, h2, _ = cols(o)
        tt = tb if ph == 0 else tb2
        for k, b, cs in ((0, r, h1), (1, l, h2)):
            rs_desc(o, ph, k).wait_recv()
            blk = rs_blk(o, ph, b, cs)
            blk[...] = (blk[...].astype(F32) + tt[o, k].astype(F32)).astype(BF16)
            rs_desc(o, ph, 4 + k).start()

    def rs_sums(o, ph):
        me = rings[(o + ph) % 2 == 0][0]
        h1, h2, _ = cols(o)
        dd, ee = (db, eb) if ph == 0 else (db2, eb2)
        for k in (2, 3, 4, 5):
            rs_desc(o, ph, k).wait_recv()
        res = []
        for cs, a, b in ((h1, ee.at[o, 0], dd.at[o, 1]), (h2, ee.at[o, 1], dd.at[o, 0])):
            blk = rs_blk(o, ph, me, cs)
            res.append((blk, cs, blk[...].astype(F32) + a[...].astype(F32) + b[...].astype(F32)))
        return res

    def ag_grp(o, ph, b, cs, c):
        if ph == 0:
            return out.at[c, b, x, :, cs] if o == 0 else out.at[c, y, b, :, cs]
        return out.at[c, :, b, :, cs] if o == 0 else out.at[c, b, :, :, cs]

    def ag_desc(o, ph, k):
        me, r, l, op, rdev, ldev = rings[(o + ph) % 2 == 1]
        h1, h2, full = cols(o)
        b, cs, to = [(me, full, rdev), (me, full, ldev), (l, h1, rdev), (r, h2, ldev)][k]
        ref = ag_grp(o, ph, b, cs, m)
        return remote(ref, ref, ags.at[o, ph, k], agr.at[o, ph, k], to)

    def dd_desc(o, k, c):
        me, r, l, op, _, _ = rings[o == 0]
        h1, h2, full = cols(o)
        b, cs = [(me, full), (l, full), (r, full), (op, h1), (op, h2)][k]
        ref = ag_grp(o, 1, b, cs, c)
        return remote(ref, ref, dds.at[o, k], ddr.at[o, k], partner)

    def wait_other():
        for o in range(2):
            for k in range(5):
                dd_desc(o, k, 1 - m).wait_recv()

    def p_desc(n):
        return remote(psnd.at[n], prcv.at[n], pss.at[n], psr.at[n], partner)

    def attention(c, l):
        a = out[c].reshape(rows, width)
        qkv = jnp.dot(a, wq[l], preferred_element_type=F32).astype(BF16)
        base = pl.multiple_of(c * rows, rows)
        kc[pl.ds(base, rows), :] = qkv[:, head:2 * head]
        vc[pl.ds(base, rows), :] = qkv[:, 2 * head:]
        s = lax.dot_general(qkv[:, :head], kc[...], (((1,), (1,)), ((), ())),
                            preferred_element_type=F32) * scale
        q_pos = base + lax.broadcasted_iota(jnp.int32, s.shape, 0)
        k_pos = lax.broadcasted_iota(jnp.int32, s.shape, 1)
        s = jnp.where(k_pos <= q_pos, s, -1e30)
        p = jnp.exp(s - jnp.max(s, axis=-1, keepdims=True))
        mix = jnp.dot(p.astype(BF16), vc[...], preferred_element_type=F32)
        ob[...] = (mix / jnp.sum(p, axis=-1, keepdims=True)).astype(BF16)

    def mlp_up(c, l):
        def body(n, carry):
            cs = pl.ds(pl.multiple_of(n * 256, 256), 256)
            a = out[c].reshape(rows, width)
            up = jnp.dot(a, wu[l, :, cs], preferred_element_type=F32)
            hid[:, cs] = jax.nn.gelu(up, approximate=True).astype(BF16)
            return carry
        lax.fori_loop(0, hid.shape[1] // 256, body, 0)

    def emit_tile(n, acc, own):
        @pl.when(own)
        def _():
            p_desc(n).wait_recv()
            total = (acc + prcv[n].astype(F32)).astype(BF16)
            cs = pl.ds(pl.multiple_of(n * tile, tile), tile)
            part[:, :, :, cs] = total.reshape(SIDE, SIDE, brow, tile)

        @pl.when(jnp.logical_not(own))
        def _():
            psnd[n] = acc.astype(BF16)
            p_desc(n).start()

    def down(o, l, odd, own):
        lo = o * (TILES // 2)

        def body(n, carry, lhs, w):
            cs = pl.ds(pl.multiple_of(n * tile, tile), tile)
            emit_tile(n, jnp.dot(lhs[...], w[l, :, cs], preferred_element_type=F32), own)
            return carry

        @pl.when(odd == 0)
        def _():
            lax.fori_loop(lo, lo + TILES // 2, functools.partial(body, lhs=ob, w=wo), 0)

        @pl.when(odd == 1)
        def _():
            lax.fori_loop(lo, lo + TILES // 2, functools.partial(body, lhs=hid, w=wd), 0)

    def slot(s, carry):
        c = lax.rem(s, CORES)
        h = lax.div(s, CORES)
        l = lax.div(h, 2)
        odd = lax.rem(h, 2)
        own = c == m
        other = c != m

        @pl.when(jnp.logical_and(other, s >= CORES))
        def _():
            wait_other()

        @pl.when(s < slots)
        def _():
            for kind in range(2):
                @pl.when(jnp.logical_and(c == 0, odd == kind))
                def _():
                    for cp in weight_copies(l, kind):
                        cp.wait()

            @pl.when(odd == 0)
            def _():
                attention(c, l)

            @pl.when(odd == 1)
            def _():
                mlp_up(c, l)

            for o in range(2):
                down(o, l, odd, own)

                @pl.when(own)
                def _():
                    rs_start(o, 0)

            @pl.when(own)
            def _():
                for o in range(2):
                    rs_fwd(o, 0)
                for o in range(2):
                    for blk, _, total in rs_sums(o, 0):
                        blk[...] = total.astype(BF16)
                    rs_start(o, 1)
                for o in range(2):
                    rs_fwd(o, 1)

        @pl.when(jnp.logical_and(other, s >= 1))
        def _():
            done = lax.div(s - 1, CORES)
            for o in range(2):
                for _, cs, total in rs_sums(o, 1):
                    xres[:, cs] = (xres[:, cs].astype(F32) + total).astype(BF16)
            xs = xres[...].astype(F32)
            gain = gains[lax.min(done + 1, halves - 1)]
            nrm = norm_rows(xs, gain)
            out[m, y, x] = jnp.where(done == halves - 1, xs, nrm).astype(BF16)
            for o in range(2):
                ag_desc(o, 0, 0).start()
                ag_desc(o, 0, 1).start()
            for o in range(2):
                for k in range(2):
                    ag_desc(o, 0, k).wait_recv()
                    ag_desc(o, 0, 2 + k).start()
            for o in range(2):
                ag_desc(o, 0, 2).wait_recv()
                ag_desc(o, 0, 3).wait_recv()
                ag_desc(o, 1, 0).start()
                ag_desc(o, 1, 1).start()
                dd_desc(o, 0, m).start()
            for o in range(2):
                for k in range(2):
                    ag_desc(o, 1, k).wait_recv()
                    ag_desc(o, 1, 2 + k).start()
                    dd_desc(o, 1 + k, m).start()
            for o in range(2):
                for k in range(2):
                    ag_desc(o, 1, 2 + k).wait_recv()
                    dd_desc(o, 3 + k, m).start()
            for o in range(2):
                for ph in range(2):
                    for k in range(6):
                        rs_desc(o, ph, k).wait_send()
                    for k in range(4):
                        ag_desc(o, ph, k).wait_send()
                for k in range(5):
                    dd_desc(o, k, m).wait_send()

            @pl.when(s < slots)
            def _():
                for n in range(TILES):
                    p_desc(n).wait_send()

        @pl.when(jnp.logical_and(other, s == 0))
        def _():
            for n in range(TILES):
                p_desc(n).wait_send()

        return carry

    lax.fori_loop(0, slots + 1, slot, 0)

    @pl.when(m == 0)
    def _():
        wait_other()


def solution(mesh):
    tp = mesh.shape["tp"]

    def device_fn(act_in, w_qkv, w_out, w_up, w_down, gain_one, gain_two):
        layers, width, _, _, head = w_qkv.shape
        seq = act_in.shape[0]
        ffn = w_up.shape[2]
        rows = seq // CORES
        brow = rows // (SIDE * SIDE)
        assert tp == SIDE * SIDE * CORES
        blocks = (CORES, SIDE, SIDE, brow, width)
        q_view = jnp.transpose(w_qkv, (0, 2, 3, 1, 4)).reshape(layers, 3, width, head)
        gains = jnp.stack([gain_one, gain_two], axis=1).reshape(2 * layers, 1, width)
        quarter = width // 4
        tile = width // TILES
        vmem = pltpu.VMEM
        dma = pltpu.SemaphoreType.DMA
        any_spec = pl.BlockSpec(memory_space=pl.ANY)
        vmem_spec = pl.BlockSpec(memory_space=pltpu.VMEM)
        big = (2, 2, SIDE, brow, quarter)
        small = (2, 2, brow, quarter)
        res = pl.pallas_call(
            stack_kernel,
            out_shape=jax.ShapeDtypeStruct(blocks, BF16),
            in_specs=[vmem_spec, any_spec, any_spec, any_spec, any_spec, vmem_spec],
            out_specs=vmem_spec,
            scratch_shapes=[
                vmem((layers, width, 3 * head), BF16),
                vmem((layers, head, width), BF16),
                vmem((layers, width, ffn), BF16),
                vmem((layers, ffn, width), BF16),
                vmem((SIDE, SIDE, brow, width), BF16),
                vmem((TILES, rows, tile), BF16),
                vmem((TILES, rows, tile), BF16),
                vmem(big, BF16), vmem(big, BF16), vmem(big, BF16),
                vmem(small, BF16), vmem(small, BF16), vmem(small, BF16),
                vmem((seq, head), BF16), vmem((seq, head), BF16),
                vmem((rows, head), BF16), vmem((rows, ffn), BF16),
                vmem((brow, width), BF16),
                dma((layers, 6)),
                dma((TILES,)), dma((TILES,)),
                dma((2, 2, 6)), dma((2, 2, 6)),
                dma((2, 2, 4)), dma((2, 2, 4)),
                dma((2, 5)), dma((2, 5)),
            ],
            compiler_params=pltpu.CompilerParams(
                collective_id=0, has_side_effects=True, vmem_limit_bytes=63 * 2 ** 20),
            name="layer_stack",
        )(act_in.reshape(blocks), q_view, w_out.reshape(layers, head, width), w_up, w_down, gains)
        return res.reshape(seq, width)

    return jax.shard_map(
        device_fn,
        mesh=mesh,
        in_specs=(
            P("dp", None),
            P(None, None, "tp", None, None),
            P(None, "tp", None, None),
            P(None, None, "tp"),
            P(None, "tp", None),
            P(None, None),
            P(None, None),
        ),
        out_specs=P("dp", None),
        check_vma=False,
    )
```

time: 739 us -> 316 us (0.43)
  waiting for transfers between devices: 608 us -> 0 us
  Pallas kernels: 0 us -> 310 us
  matrix products: 63.4 us -> 0 us
  other arithmetic: 46.3 us -> 0.9 us
  between operations: 14 us -> 0.02 us
    psum x6 -> x0, waiting for transfers between devices: 608 us -> none  [the longest x3 306 us: device_fn(): attn_sum = lax.psum(part_sum, 'tp')]
    pallas_call x0 -> x1, Pallas kernels: none -> 310 us  [device_fn(): pl.pallas_call(stack_kernel, out_shape=jax.ShapeDtypeStruct(blocks, BF16)...]
    dot_general x15 -> x0, matrix products: 63.4 us -> none  [the longest x3 19.8 us: device_fn(): jnp.dot(hidden, w_down[layer_idx], preferred_element_type=jnp.float32)]
    reduce_sum x15 -> x0, other arithmetic: 38.9 us -> none  [the longest x6 28.8 us: layer_norm(): centred = rows_f32 - jnp.mean(rows_f32, axis=-1, keepdims=True)]
  transfers between devices with their start and end apart: 6 -> 0, of which waited for: 6 -> 0; matrix products, arithmetic and copies ran while one was open for 0% -> 0% of each run, Pallas kernels for 0% -> 0%
where the time goes in v1:
time: 316 us
  Pallas kernels  310 us (98%)
  local copies, waits for them, and re-layouts  5.57 us (2%)
    pallas_call x1, Pallas kernels, device_fn(): pl.pallas_call(stack_kernel, out_shape=jax.ShapeDtypeStruct(blocks, BF16)...  310 us

profile of v1, /device:TPU:97, one launch (start us, length us, event | category | flops | bytes accessed | tf_op | source)
XLA Modules:
  0.0 316.0 jit_solution(14181123642809299820)
XLA Ops:
  0.0 0.9 pad_maximum_fusion
  0.9 0.1 copy.9
  1.0 0.8 reshape.18.gains
  1.8 309.5 %layer_stack.1 = bf16[2,4,4,16,4096]{4,3,2,1,0:T(8,128)(2,1)} custom-call(bf16[2,4,4,16,4096]{4,3,2,1,0:T(8,128)(2,1)} %bitcast.12, bf16[3,3,4096,128]{3,2,1,0:T(8,128)(2,1)} %bitcast.11, bf16[3,128,4096]{2,1,0:T(8,128)(2,1)} %bitcast.13, bf16[3,4096,512]{2,1,0:T(8,128)(2,1)} %hu.1, bf16[3,512,4096]{2,1,0:T(8,128)(2,1)} %hd.1, f32[6,1,4096]{2,1,0:T(1,128)} %reshape.18.gains), custom_call_target="tpu_custom_call" | custom-call | tf_op jit(solution)/shard_map/layer_stack/pallas_call | solution.py:348
  311.3 4.7 %copy.11 = bf16[512,4096]{1,0:T(8,128)(2,1)} copy(bf16[512,4096]{1,0:T(8,128)(2,1)} %bitcast.10) | data formatting | bytes 8388608

commit v2 on v1

--- a/solution.py
+++ b/solution.py
@@ -80,7 +80,8 @@
         out[c, b] = norm_rows(act[c, b].astype(F32), gains[0]).astype(BF16)
         return carry
 
-    lax.fori_loop(0, CORES * SIDE, first_norm, 0)
+    with jax.named_scope("first_norm"):
+        lax.fori_loop(0, CORES * SIDE, first_norm, 0)
     xres[...] = act[m, y, x]
 
     pl.semaphore_wait(barrier, len(peers))
@@ -97,70 +98,129 @@
         h2 = pl.ds((2 * o + 1) * quarter, quarter)
         return h1, h2, pl.ds(2 * o * quarter, 2 * quarter)
 
-    def rs_blk(o, ph, b, cs):
-        if ph == 0:
-            return part.at[:, b, :, cs] if o == 0 else part.at[b, :, :, cs]
-        return part.at[b, x, :, cs] if o == 0 else part.at[y, b, :, cs]
-
-    def rs_desc(o, ph, k):
-        me, r, l, op, rdev, ldev = rings[(o + ph) % 2 == 0]
-        h1, h2, _ = cols(o)
-        tt, dd, ee = (tb, db, eb) if ph == 0 else (tb2, db2, eb2)
+    first = [rings[True], rings[False]]
+    second = [rings[False], rings[True]]
+
+    def b2_of(o, p):
+        me2, r2, l2, op2, _, _ = second[o]
+        return (op2, r2, l2, me2)[p]
+
+    def rs_blk(o, b1, b2, cs):
+        return part.at[b2, b1, :, cs] if o == 0 else part.at[b1, b2, :, cs]
+
+    def rs1(o, p, k):
+        _, r, l, op, rdev, ldev = first[o]
+        h1, h2, _ = cols(o)
         b, cs, dst, to = [
-            (op, h1, tt.at[o, 0], rdev), (op, h2, tt.at[o, 1], ldev),
-            (r, h2, dd.at[o, 0], rdev), (l, h1, dd.at[o, 1], ldev),
-            (r, h1, ee.at[o, 0], rdev), (l, h2, ee.at[o, 1], ldev)][k]
-        return remote(rs_blk(o, ph, b, cs), dst, rss.at[o, ph, k], rsr.at[o, ph, k], to)
-
-    def rs_start(o, ph):
-        for k in range(4):
-            rs_desc(o, ph, k).start()
-
-    def rs_fwd(o, ph):
-        _, r, l, _, _, _ = rings[(o + ph) % 2 == 0]
-        h1, h2, _ = cols(o)
-        tt = tb if ph == 0 else tb2
+            (op, h1, tb.at[o, 0, p], rdev), (op, h2, tb.at[o, 1, p], ldev),
+            (r, h2, db.at[o, 0, p], rdev), (l, h1, db.at[o, 1, p], ldev),
+            (r, h1, eb.at[o, 0, p], rdev), (l, h2, eb.at[o, 1, p], ldev)][k]
+        return remote(rs_blk(o, b, b2_of(o, p), cs), dst, rss.at[o, p, k], rsr.at[o, p, k], to)
+
+    def rs2(o, k):
+        me1 = first[o][0]
+        _, r, l, op, rdev, ldev = second[o]
+        h1, h2, _ = cols(o)
+        b, cs, dst, to = [
+            (op, h1, tb2.at[o, 0], rdev), (op, h2, tb2.at[o, 1], ldev),
+            (r, h2, db2.at[o, 0], rdev), (l, h1, db2.at[o, 1], ldev),
+            (r, h1, eb2.at[o, 0], rdev), (l, h2, eb2.at[o, 1], ldev)][k]
+        return remote(rs_blk(o, me1, b, cs), dst, rss.at[o, 4, k], rsr.at[o, 4, k], to)
+
+    def add_to(blk, *others):
+        total = blk[...].astype(F32)
+        for other in others:
+            total = total + other[...].astype(F32)
+        return total
+
+    def rs1_start(o):
+        for ks in ((0, 1), (2, 3)):
+            for p in range(SIDE):
+                for k in ks:
+                    rs1(o, p, k).start()
+
+    def rs1_forward(o, p):
+        _, r, l, _, _, _ = first[o]
+        h1, h2, _ = cols(o)
         for k, b, cs in ((0, r, h1), (1, l, h2)):
-            rs_desc(o, ph, k).wait_recv()
-            blk = rs_blk(o, ph, b, cs)
-            blk[...] = (blk[...].astype(F32) + tt[o, k].astype(F32)).astype(BF16)
-            rs_desc(o, ph, 4 + k).start()
-
-    def rs_sums(o, ph):
-        me = rings[(o + ph) % 2 == 0][0]
-        h1, h2, _ = cols(o)
-        dd, ee = (db, eb) if ph == 0 else (db2, eb2)
+            rs1(o, p, k).wait_recv()
+            blk = rs_blk(o, b, b2_of(o, p), cs)
+            blk[...] = add_to(blk, tb.at[o, k, p]).astype(BF16)
+            rs1(o, p, 4 + k).start()
+
+    def rs1_sum(o, p):
+        h1, h2, _ = cols(o)
         for k in (2, 3, 4, 5):
-            rs_desc(o, ph, k).wait_recv()
-        res = []
-        for cs, a, b in ((h1, ee.at[o, 0], dd.at[o, 1]), (h2, ee.at[o, 1], dd.at[o, 0])):
-            blk = rs_blk(o, ph, me, cs)
-            res.append((blk, cs, blk[...].astype(F32) + a[...].astype(F32) + b[...].astype(F32)))
-        return res
-
-    def ag_grp(o, ph, b, cs, c):
-        if ph == 0:
-            return out.at[c, b, x, :, cs] if o == 0 else out.at[c, y, b, :, cs]
-        return out.at[c, :, b, :, cs] if o == 0 else out.at[c, b, :, :, cs]
-
-    def ag_desc(o, ph, k):
-        me, r, l, op, rdev, ldev = rings[(o + ph) % 2 == 1]
+            rs1(o, p, k).wait_recv()
+        for cs, a, b in ((h1, eb.at[o, 0, p], db.at[o, 1, p]), (h2, eb.at[o, 1, p], db.at[o, 0, p])):
+            blk = rs_blk(o, first[o][0], b2_of(o, p), cs)
+            blk[...] = add_to(blk, a, b).astype(BF16)
+        for k in ((0, 1), (2,), (3,), ())[p]:
+            rs2(o, k).start()
+
+    def rs2_forward(o):
+        _, r, l, _, _, _ = second[o]
+        h1, h2, _ = cols(o)
+        for k, b, cs in ((0, r, h1), (1, l, h2)):
+            rs2(o, k).wait_recv()
+            blk = rs_blk(o, first[o][0], b, cs)
+            blk[...] = add_to(blk, tb2.at[o, k]).astype(BF16)
+            rs2(o, 4 + k).start()
+
+    def rs2_sum(o):
+        h1, h2, _ = cols(o)
+        for k in (2, 3, 4, 5):
+            rs2(o, k).wait_recv()
+        for cs, a, b in ((h1, eb2.at[o, 0], db2.at[o, 1]), (h2, eb2.at[o, 1], db2.at[o, 0])):
+            blk = rs_blk(o, first[o][0], second[o][0], cs)
+            xres[:, cs] = add_to(xres.at[:, cs], blk, a, b).astype(BF16)
+
+    def ag_blk(o, b1, b2, cs):
+        return out.at[m, b2, b1, :, cs] if o == 0 else out.at[m, b1, b2, :, cs]
+
+    def ag1(o, k):
+        me1 = first[o][0]
+        me, r, l, _, rdev, ldev = second[o]
         h1, h2, full = cols(o)
         b, cs, to = [(me, full, rdev), (me, full, ldev), (l, h1, rdev), (r, h2, ldev)][k]
-        ref = ag_grp(o, ph, b, cs, m)
-        return remote(ref, ref, ags.at[o, ph, k], agr.at[o, ph, k], to)
-
-    def dd_desc(o, k, c):
-        me, r, l, op, _, _ = rings[o == 0]
+        ref = ag_blk(o, me1, b, cs)
+        return remote(ref, ref, ags.at[o, 4, k], agr.at[o, 4, k], to)
+
+    def ag2(o, p, k):
+        me, r, l, _, rdev, ldev = first[o]
+        h1, h2, full = cols(o)
+        b, cs, to = [(me, full, rdev), (me, full, ldev), (l, h1, rdev), (r, h2, ldev)][k]
+        ref = ag_blk(o, b, b2_of(o, p), cs)
+        return remote(ref, ref, ags.at[o, p, k], agr.at[o, p, k], to)
+
+    def to_partner(o, k, p):
+        me, r, l, op, _, _ = first[o]
         h1, h2, full = cols(o)
         b, cs = [(me, full), (l, full), (r, full), (op, h1), (op, h2)][k]
-        ref = ag_grp(o, 1, b, cs, c)
-        return remote(ref, ref, dds.at[o, k], ddr.at[o, k], partner)
+        ref = ag_blk(o, b, b2_of(o, p), cs)
+        remote(ref, ref, dds.at[0], ddr.at[0], partner).start()
+
+    def whole(c):
+        return remote(out.at[c], out.at[c], dds.at[0], ddr.at[0], partner)
 
     def wait_other():
-        for o in range(2):
-            for k in range(5):
-                dd_desc(o, k, 1 - m).wait_recv()
+        whole(1 - m).wait_recv()
+
+    def gather_piece(o, p):
+        ag2(o, p, 0).start()
+        ag2(o, p, 1).start()
+        to_partner(o, 0, p)
+
+    def gather_forward(o, p):
+        for k in range(2):
+            ag2(o, p, k).wait_recv()
+            ag2(o, p, 2 + k).start()
+            to_partner(o, 1 + k, p)
+
+    def gather_end(o, p):
+        for k in range(2):
+            ag2(o, p, 2 + k).wait_recv()
+            to_partner(o, 3 + k, p)
 
     def p_desc(n):
         return remote(psnd.at[n], prcv.at[n], pss.at[n], psr.at[n], partner)
@@ -218,6 +278,80 @@
         def _():
             lax.fori_loop(lo, lo + TILES // 2, functools.partial(body, lhs=hid, w=wd), 0)
 
+    def scatter_first():
+        with jax.named_scope("rs1"):
+            for p in range(2):
+                for o in range(2):
+                    rs1_forward(o, p)
+            for p in range(2, SIDE):
+                for o in range(2):
+                    rs1_sum(o, p - 2)
+                    rs1_forward(o, p)
+        with jax.named_scope("rs1_end"):
+            for p in (2, 3):
+                for o in range(2):
+                    rs1_sum(o, p)
+
+    def owned_norm(done):
+        with jax.named_scope("rs2_sum"):
+            for o in range(2):
+                rs2_sum(o)
+        with jax.named_scope("owned_norm"):
+            xs = xres[...].astype(F32)
+            gain = gains[lax.min(done + 1, halves - 1)]
+            nrm = norm_rows(xs, gain)
+            out[m, y, x] = jnp.where(done == halves - 1, xs, nrm).astype(BF16)
+
+    def gather():
+        both = range(2)
+        with jax.named_scope("ag1"):
+            for o in both:
+                ag1(o, 0).start()
+                ag1(o, 1).start()
+            for o in both:
+                gather_piece(o, 3)
+            for k in range(2):
+                for o in both:
+                    ag1(o, k).wait_recv()
+                    ag1(o, 2 + k).start()
+                    gather_piece(o, 2 - k)
+        with jax.named_scope("ag2_me"):
+            for o in both:
+                gather_forward(o, 3)
+        with jax.named_scope("ag1_end"):
+            for o in both:
+                ag1(o, 2).wait_recv()
+                ag1(o, 3).wait_recv()
+                gather_piece(o, 0)
+        with jax.named_scope("ag2_side"):
+            for p in (2, 1):
+                for o in both:
+                    gather_forward(o, p)
+        with jax.named_scope("ag2_me_end"):
+            for o in both:
+                gather_end(o, 3)
+        with jax.named_scope("ag2_op"):
+            for o in both:
+                gather_forward(o, 0)
+        with jax.named_scope("ag2_end"):
+            for p in (2, 1, 0):
+                for o in both:
+                    gather_end(o, p)
+
+    def drain():
+        with jax.named_scope("drain"):
+            for o in range(2):
+                for p in range(SIDE):
+                    for k in range(6):
+                        rs1(o, p, k).wait_send()
+                    for k in range(4):
+                        ag2(o, p, k).wait_send()
+                for k in range(6):
+                    rs2(o, k).wait_send()
+                for k in range(4):
+                    ag1(o, k).wait_send()
+            whole(m).wait_send()
+
     def slot(s, carry):
         c = lax.rem(s, CORES)
         h = lax.div(s, CORES)
@@ -225,92 +359,52 @@
         odd = lax.rem(h, 2)
         own = c == m
         other = c != m
+        closing = jnp.logical_and(other, s >= 1)
+        inside = s < slots
 
         @pl.when(jnp.logical_and(other, s >= CORES))
         def _():
-            wait_other()
-
-        @pl.when(s < slots)
-        def _():
-            for kind in range(2):
-                @pl.when(jnp.logical_and(c == 0, odd == kind))
+            with jax.named_scope("wait_other"):
+                wait_other()
+
+        for kind in range(2):
+            @pl.when(jnp.logical_and(inside, odd == kind))
+            def _():
+                @pl.when(c == 0)
                 def _():
                     for cp in weight_copies(l, kind):
                         cp.wait()
 
-            @pl.when(odd == 0)
+                with jax.named_scope("up"):
+                    (attention, mlp_up)[kind](c, l)
+
+        @pl.when(closing)
+        def _():
+            with jax.named_scope("rs2_forward"):
+                for o in range(2):
+                    rs2_forward(o)
+
+        for o in range(2):
+            @pl.when(inside)
             def _():
-                attention(c, l)
-
-            @pl.when(odd == 1)
+                with jax.named_scope("down"):
+                    down(o, l, odd, own)
+
+            @pl.when(jnp.logical_and(inside, own))
             def _():
-                mlp_up(c, l)
-
-            for o in range(2):
-                down(o, l, odd, own)
-
-                @pl.when(own)
-                def _():
-                    rs_start(o, 0)
-
-            @pl.when(own)
-            def _():
-                for o in range(2):
-                    rs_fwd(o, 0)
-                for o in range(2):
-                    for blk, _, total in rs_sums(o, 0):
-                        blk[...] = total.astype(BF16)
-                    rs_start(o, 1)
-                for o in range(2):
-                    rs_fwd(o, 1)
-
-        @pl.when(jnp.logical_and(other, s >= 1))
-        def _():
-            done = lax.div(s - 1, CORES)
-            for o in range(2):
-                for _, cs, total in rs_sums(o, 1):
-                    xres[:, cs] = (xres[:, cs].astype(F32) + total).astype(BF16)
-            xs = xres[...].astype(F32)
-            gain = gains[lax.min(done + 1, halves - 1)]
-            nrm = norm_rows(xs, gain)
-            out[m, y, x] = jnp.where(done == halves - 1, xs, nrm).astype(BF16)
-            for o in range(2):
-                ag_desc(o, 0, 0).start()
-                ag_desc(o, 0, 1).start()
-            for o in range(2):
-                for k in range(2):
-                    ag_desc(o, 0, k).wait_recv()
-                    ag_desc(o, 0, 2 + k).start()
-            for o in range(2):
-                ag_desc(o, 0, 2).wait_recv()
-                ag_desc(o, 0, 3).wait_recv()
-                ag_desc(o, 1, 0).start()
-                ag_desc(o, 1, 1).start()
-                dd_desc(o, 0, m).start()
-            for o in range(2):
-                for k in range(2):
-                    ag_desc(o, 1, k).wait_recv()
-                    ag_desc(o, 1, 2 + k).start()
-                    dd_desc(o, 1 + k, m).start()
-            for o in range(2):
-                for k in range(2):
-                    ag_desc(o, 1, 2 + k).wait_recv()
-                    dd_desc(o, 3 + k, m).start()
-            for o in range(2):
-                for ph in range(2):
-                    for k in range(6):
-                        rs_desc(o, ph, k).wait_send()
-                    for k in range(4):
-                        ag_desc(o, ph, k).wait_send()
-                for k in range(5):
-                    dd_desc(o, k, m).wait_send()
-
-            @pl.when(s < slots)
-            def _():
-                for n in range(TILES):
-                    p_desc(n).wait_send()
-
-        @pl.when(jnp.logical_and(other, s == 0))
+                rs1_start(o)
+
+        @pl.when(jnp.logical_and(inside, own))
+        def _():
+            scatter_first()
+
+        @pl.when(closing)
+        def _():
+            owned_norm(lax.div(s - 1, CORES))
+            gather()
+            drain()
+
+        @pl.when(jnp.logical_and(inside, other))
         def _():
             for n in range(TILES):
                 p_desc(n).wait_send()
@@ -365,9 +459,9 @@
                 vmem((brow, width), BF16),
                 dma((layers, 6)),
                 dma((TILES,)), dma((TILES,)),
-                dma((2, 2, 6)), dma((2, 2, 6)),
-                dma((2, 2, 4)), dma((2, 2, 4)),
-                dma((2, 5)), dma((2, 5)),
+                dma((2, SIDE + 1, 6)), dma((2, SIDE + 1, 6)),
+                dma((2, SIDE + 1, 4)), dma((2, SIDE + 1, 4)),
+                dma((1,)), dma((1,)),
             ],
             compiler_params=pltpu.CompilerParams(
                 collective_id=0, has_side_effects=True, vmem_limit_bytes=63 * 2 ** 20),

time: 316 us -> 296 us (0.937)
  Pallas kernels: 310 us -> 290 us
    pallas_call x1, Pallas kernels: 310 us -> 290 us  [device_fn(): pl.pallas_call(stack_kernel, out_shape=jax.ShapeDtypeStruct(blocks, BF16)...]
where the time goes in v2:
time: 296 us
  Pallas kernels  290 us (98%)
  local copies, waits for them, and re-layouts  5.57 us (2%)
    pallas_call x1, Pallas kernels, device_fn(): pl.pallas_call(stack_kernel, out_shape=jax.ShapeDtypeStruct(blocks, BF16)...  290 us

profile of v2, /device:TPU:97, one launch (start us, length us, event | category | flops | bytes accessed | tf_op | source)
XLA Modules:
  0.0 296.3 jit_solution(13773280686692255259)
XLA Ops:
  0.0 0.9 pad_maximum_fusion
  0.9 0.1 copy.9
  1.0 0.8 reshape.18.gains
  1.8 289.8 %layer_stack.1 = bf16[2,4,4,16,4096]{4,3,2,1,0:T(8,128)(2,1)} custom-call(bf16[2,4,4,16,4096]{4,3,2,1,0:T(8,128)(2,1)} %bitcast.12, bf16[3,3,4096,128]{3,2,1,0:T(8,128)(2,1)} %bitcast.11, bf16[3,128,4096]{2,1,0:T(8,128)(2,1)} %bitcast.13, bf16[3,4096,512]{2,1,0:T(8,128)(2,1)} %hu.1, bf16[3,512,4096]{2,1,0:T(8,128)(2,1)} %hd.1, f32[6,1,4096]{2,1,0:T(1,128)} %reshape.18.gains), custom_call_target="tpu_custom_call" | custom-call | tf_op jit(solution)/shard_map/layer_stack/pallas_call | solution.py:442
  291.6 4.7 %copy.11 = bf16[512,4096]{1,0:T(8,128)(2,1)} copy(bf16[512,4096]{1,0:T(8,128)(2,1)} %bitcast.10) | data formatting | bytes 8388608

commit v3 on v2

v3 whole, which is shorter than its diff:
```python
import functools
import math
import jax
import jax.numpy as jnp
from jax import lax
from jax.experimental import pallas as pl
from jax.experimental.pallas import tpu as pltpu
from jax.sharding import PartitionSpec as P

F32 = jnp.float32
BF16 = jnp.bfloat16
SIDE = 4
CORES = 2
TILES = 8


def norm_rows(rows, gain):
    centred = rows - jnp.mean(rows, axis=-1, keepdims=True)
    var = jnp.mean(centred * centred, axis=-1, keepdims=True)
    return centred * lax.rsqrt(var + 1e-5) * gain


def stack_kernel(act, hq, ho, hu, hd, gains, out,
                 wq, wo, wu, wd, part, psnd, prcv, fb, gb,
                 kc, vc, ob, hid, xres,
                 wsem, pss, psr, rss, rsr, ags, agr, dds, ddr):
    layers = hq.shape[0]
    rows = act.shape[1] * act.shape[2] * act.shape[3]
    brow = act.shape[3]
    width = act.shape[4]
    head = hq.shape[3]
    tile = width // TILES
    halves = 2 * layers
    slots = CORES * halves
    scale = 1.0 / math.sqrt(head)

    t = lax.axis_index("tp")
    z = lax.axis_index("dp")
    m = lax.rem(t, CORES)
    x = lax.rem(lax.div(t, CORES), SIDE)
    y = lax.div(t, CORES * SIDE)
    partner = t + 1 - 2 * m

    def dev(yy, xx):
        return (yy * SIDE + xx) * CORES + m

    def ring(along_x):
        me = x if along_x else y
        r, o, l = (lax.rem(me + k, SIDE) for k in (1, 2, 3))
        if along_x:
            return me, r, l, o, dev(y, r), dev(y, l), dev(y, o)
        return me, r, l, o, dev(r, x), dev(l, x), dev(o, x)

    rings = {True: ring(True), False: ring(False)}

    barrier = pltpu.get_barrier_semaphore()
    peers = [partner, *rings[True][4:], *rings[False][4:]]
    for peer in peers:
        pl.semaphore_signal(barrier, inc=1, device_id=(z, peer), device_id_type=pl.DeviceIdType.MESH)

    def weight_copies(l, kind):
        if kind == 0:
            cps = [pltpu.make_async_copy(
                hq.at[l, c], wq.at[l, :, pl.ds(c * head, head)], wsem.at[l, c]) for c in range(3)]
            return cps + [pltpu.make_async_copy(ho.at[l], wo.at[l], wsem.at[l, 3])]
        return [pltpu.make_async_copy(hu.at[l], wu.at[l], wsem.at[l, 4]),
                pltpu.make_async_copy(hd.at[l], wd.at[l], wsem.at[l, 5])]

    for l in range(layers):
        for kind in range(2):
            for cp in weight_copies(l, kind):
                cp.start()

    kc[...] = jnp.zeros_like(kc)
    vc[...] = jnp.zeros_like(vc)

    def first_norm(i, carry):
        c = lax.div(i, SIDE)
        b = lax.rem(i, SIDE)
        out[c, b] = norm_rows(act[c, b].astype(F32), gains[0]).astype(BF16)
        return carry

    with jax.named_scope("first_norm"):
        lax.fori_loop(0, CORES * SIDE, first_norm, 0)
    xres[...] = act[m, y, x]

    pl.semaphore_wait(barrier, len(peers))

    def remote(src, dst, ss, rs, peer):
        return pltpu.make_async_remote_copy(
            src_ref=src, dst_ref=dst, send_sem=ss, recv_sem=rs,
            device_id=(z, peer), device_id_type=pl.DeviceIdType.MESH)

    half = width // 2

    def cols(o):
        return pl.ds(o * half, half)

    first = [rings[True], rings[False]]
    second = [rings[False], rings[True]]

    def b2_of(o, p):
        me2, r2, l2, op2 = second[o][:4]
        return (op2, r2, l2, me2)[p]

    def rs_blk(o, b1, b2, cs):
        return part.at[b2, b1, :, cs] if o == 0 else part.at[b1, b2, :, cs]

    def rs1(o, p, k):
        _, r, l, op, rdev, ldev, opdev = first[o]
        b, to = [(op, opdev), (r, rdev), (l, ldev)][k]
        src = rs_blk(o, b, b2_of(o, p), cols(o))
        return remote(src, fb.at[o, k, p], rss.at[o, p, k], rsr.at[o, p, k], to)

    def rs2(o, k):
        _, r, l, op, rdev, ldev, opdev = second[o]
        b, to = [(op, opdev), (r, rdev), (l, ldev)][k]
        return remote(rs_blk(o, first[o][0], b, cols(o)), gb.at[o, k], rss.at[o, 4, k], rsr.at[o, 4, k], to)

    def add_to(blk, *others):
        total = blk[...].astype(F32)
        for other in others:
            total = total + other[...].astype(F32)
        return total

    def rs1_start(o):
        for p in range(SIDE):
            for k in range(3):
                rs1(o, p, k).start()

    def rs1_sum(o, p):
        for k in range(3):
            rs1(o, p, k).wait_recv()
        blk = rs_blk(o, first[o][0], b2_of(o, p), cols(o))
        blk[...] = add_to(blk, *(fb.at[o, k, p] for k in range(3))).astype(BF16)
        if p < 3:
            rs2(o, p).start()

    def rs2_sum(o):
        full = cols(o)
        for k in range(3):
            rs2(o, k).wait_recv()
        blk = rs_blk(o, first[o][0], second[o][0], full)
        xres[:, full] = add_to(xres.at[:, full], blk, *(gb.at[o, k] for k in range(3))).astype(BF16)

    def ag_blk(o, b1, b2, cs):
        return out.at[m, b2, b1, :, cs] if o == 0 else out.at[m, b1, b2, :, cs]

    def ag1(o, k):
        to = second[o][4 + (2, 0, 1)[k]]
        ref = ag_blk(o, first[o][0], second[o][0], cols(o))
        return remote(ref, ref, ags.at[o, 4, k], agr.at[o, 4, k], to)

    def ag2(o, p, k):
        to = first[o][4 + (2, 0, 1)[k]]
        ref = ag_blk(o, first[o][0], b2_of(o, p), cols(o))
        return remote(ref, ref, ags.at[o, p, k], agr.at[o, p, k], to)

    def to_partner(o, b, p):
        ref = ag_blk(o, b, b2_of(o, p), cols(o))
        remote(ref, ref, dds.at[0], ddr.at[0], partner).start()

    def whole(c):
        return remote(out.at[c], out.at[c], dds.at[0], ddr.at[0], partner)

    def wait_other():
        whole(1 - m).wait_recv()

    def gather_piece(o, p):
        for k in range(3):
            ag2(o, p, k).start()
        to_partner(o, first[o][0], p)

    def p_desc(n):
        return remote(psnd.at[n], prcv.at[n], pss.at[n], psr.at[n], partner)

    def attention(c, l):
        a = out[c].reshape(rows, width)
        qkv = jnp.dot(a, wq[l], preferred_element_type=F32).astype(BF16)
        base = pl.multiple_of(c * rows, rows)
        kc[pl.ds(base, rows), :] = qkv[:, head:2 * head]
        vc[pl.ds(base, rows), :] = qkv[:, 2 * head:]
        s = lax.dot_general(qkv[:, :head], kc[...], (((1,), (1,)), ((), ())),
                            preferred_element_type=F32) * scale
        q_pos = base + lax.broadcasted_iota(jnp.int32, s.shape, 0)
        k_pos = lax.broadcasted_iota(jnp.int32, s.shape, 1)
        s = jnp.where(k_pos <= q_pos, s, -1e30)
        p = jnp.exp(s - jnp.max(s, axis=-1, keepdims=True))
        mix = jnp.dot(p.astype(BF16), vc[...], preferred_element_type=F32)
        ob[...] = (mix / jnp.sum(p, axis=-1, keepdims=True)).astype(BF16)

    def mlp_up(c, l):
        def body(n, carry):
            cs = pl.ds(pl.multiple_of(n * 256, 256), 256)
            a = out[c].reshape(rows, width)
            up = jnp.dot(a, wu[l, :, cs], preferred_element_type=F32)
            hid[:, cs] = jax.nn.gelu(up, approximate=True).astype(BF16)
            return carry
        lax.fori_loop(0, hid.shape[1] // 256, body, 0)

    def emit_tile(n, acc, own):
        @pl.when(own)
        def _():
            p_desc(n).wait_recv()
            total = (acc + prcv[n].astype(F32)).astype(BF16)
            cs = pl.ds(pl.multiple_of(n * tile, tile), tile)
            part[:, :, :, cs] = total.reshape(SIDE, SIDE, brow, tile)

        @pl.when(jnp.logical_not(own))
        def _():
            psnd[n] = acc.astype(BF16)
            p_desc(n).start()

    def down(o, l, odd, own):
        lo = o * (TILES // 2)

        def body(n, carry, lhs, w):
            cs = pl.ds(pl.multiple_of(n * tile, tile), tile)
            emit_tile(n, jnp.dot(lhs[...], w[l, :, cs], preferred_element_type=F32), own)
            return carry

        @pl.when(odd == 0)
        def _():
            lax.fori_loop(lo, lo + TILES // 2, functools.partial(body, lhs=ob, w=wo), 0)

        @pl.when(odd == 1)
        def _():
            lax.fori_loop(lo, lo + TILES // 2, functools.partial(body, lhs=hid, w=wd), 0)

    def reduce_and_norm(done):
        for p in range(SIDE):
            with jax.named_scope(f"rs1_sum{p}"):
                for o in range(2):
                    rs1_sum(o, p)
        with jax.named_scope("rs2_sum"):
            for o in range(2):
                rs2_sum(o)
        with jax.named_scope("owned_norm"):
            xs = xres[...].astype(F32)
            gain = gains[lax.min(done + 1, halves - 1)]
            nrm = norm_rows(xs, gain)
            out[m, y, x] = jnp.where(done == halves - 1, xs, nrm).astype(BF16)

    def gather_start():
        with jax.named_scope("ag1"):
            for k in range(3):
                for o in range(2):
                    ag1(o, k).start()
            for o in range(2):
                gather_piece(o, 3)
        for k in (1, 2, 0):
            with jax.named_scope(f"ag1_{k}"):
                for o in range(2):
                    ag1(o, k).wait_recv()
                    gather_piece(o, (0, 2, 1)[k])

    def gather_end():
        for p in (3, 2, 1, 0):
            with jax.named_scope(f"ag2_{p}"):
                for o in range(2):
                    for k in range(3):
                        ag2(o, p, k).wait_recv()
                        to_partner(o, first[o][(3, 2, 1)[k]], p)

    def drain():
        with jax.named_scope("drain"):
            for o in range(2):
                for k in range(3):
                    for p in range(SIDE):
                        rs1(o, p, k).wait_send()
                        ag2(o, p, k).wait_send()
                    rs2(o, k).wait_send()
                    ag1(o, k).wait_send()
            whole(m).wait_send()

    def slot(s, carry):
        c = lax.rem(s, CORES)
        h = lax.div(s, CORES)
        l = lax.div(h, 2)
        odd = lax.rem(h, 2)
        own = c == m
        other = c != m
        inside = s < slots

        @pl.when(jnp.logical_and(other, s >= CORES))
        def _():
            with jax.named_scope("wait_other"):
                wait_other()

        for kind in range(2):
            @pl.when(jnp.logical_and(inside, odd == kind))
            def _():
                @pl.when(c == 0)
                def _():
                    for cp in weight_copies(l, kind):
                        cp.wait()

                with jax.named_scope("up"):
                    (attention, mlp_up)[kind](c, l)

        @pl.when(jnp.logical_and(jnp.logical_and(inside, own), s >= CORES))
        def _():
            drain()

        for o in range(2):
            @pl.when(inside)
            def _():
                with jax.named_scope("down"):
                    down(o, l, odd, own)

            @pl.when(jnp.logical_and(inside, own))
            def _():
                rs1_start(o)

        @pl.when(c == 1)
        def _():
            reduce_and_norm(h)
            gather_start()

        @pl.when(jnp.logical_and(s >= 1, other))
        def _():
            gather_end()

        @pl.when(jnp.logical_and(inside, other))
        def _():
            for n in range(TILES):
                p_desc(n).wait_send()

        return carry

    lax.fori_loop(0, slots + 1, slot, 0)
    drain()

    @pl.when(m == 0)
    def _():
        wait_other()


def solution(mesh):
    tp = mesh.shape["tp"]

    def device_fn(act_in, w_qkv, w_out, w_up, w_down, gain_one, gain_two):
        layers, width, _, _, head = w_qkv.shape
        seq = act_in.shape[0]
        ffn = w_up.shape[2]
        rows = seq // CORES
        brow = rows // (SIDE * SIDE)
        assert tp == SIDE * SIDE * CORES
        blocks = (CORES, SIDE, SIDE, brow, width)
        q_view = jnp.transpose(w_qkv, (0, 2, 3, 1, 4)).reshape(layers, 3, width, head)
        gains = jnp.stack([gain_one, gain_two], axis=1).reshape(2 * layers, 1, width)
        half = width // 2
        tile = width // TILES
        vmem = pltpu.VMEM
        dma = pltpu.SemaphoreType.DMA
        any_spec = pl.BlockSpec(memory_space=pl.ANY)
        vmem_spec = pl.BlockSpec(memory_space=pltpu.VMEM)
        res = pl.pallas_call(
            stack_kernel,
            out_shape=jax.ShapeDtypeStruct(blocks, BF16),
            in_specs=[vmem_spec, any_spec, any_spec, any_spec, any_spec, vmem_spec],
            out_specs=vmem_spec,
            scratch_shapes=[
                vmem((layers, width, 3 * head), BF16),
                vmem((layers, head, width), BF16),
                vmem((layers, width, ffn), BF16),
                vmem((layers, ffn, width), BF16),
                vmem((SIDE, SIDE, brow, width), BF16),
                vmem((TILES, rows, tile), BF16),
                vmem((TILES, rows, tile), BF16),
                vmem((2, 3, SIDE, brow, half), BF16),
                vmem((2, 3, brow, half), BF16),
                vmem((seq, head), BF16), vmem((seq, head), BF16),
                vmem((rows, head), BF16), vmem((rows, ffn), BF16),
                vmem((brow, width), BF16),
                dma((layers, 6)),
                dma((TILES,)), dma((TILES,)),
                dma((2, SIDE + 1, 3)), dma((2, SIDE + 1, 3)),
                dma((2, SIDE + 1, 3)), dma((2, SIDE + 1, 3)),
                dma((1,)), dma((1,)),
            ],
            compiler_params=pltpu.CompilerParams(
                collective_id=0, has_side_effects=True, vmem_limit_bytes=63 * 2 ** 20),
            name="layer_stack",
        )(act_in.reshape(blocks), q_view, w_out.reshape(layers, head, width), w_up, w_down, gains)
        return res.reshape(seq, width)

    return jax.shard_map(
        device_fn,
        mesh=mesh,
        in_specs=(
            P("dp", None),
            P(None, None, "tp", None, None),
            P(None, "tp", None, None),
            P(None, None, "tp"),
            P(None, "tp", None),
            P(None, None),
            P(None, None),
        ),
        out_specs=P("dp", None),
        check_vma=False,
    )
```

time: 296 us -> 247 us (0.83)
  Pallas kernels: 290 us -> 240 us
    pallas_call x1, Pallas kernels: 290 us -> 240 us  [device_fn(): pl.pallas_call(stack_kernel, out_shape=jax.ShapeDtypeStruct(blocks, BF16)...]
where the time goes in v3:
time: 247 us
  Pallas kernels  240 us (97%)
  local copies, waits for them, and re-layouts  5.57 us (2%)
    pallas_call x1, Pallas kernels, device_fn(): pl.pallas_call(stack_kernel, out_shape=jax.ShapeDtypeStruct(blocks, BF16)...  240 us

profile of v3, /device:TPU:97, one launch (start us, length us, event | category | flops | bytes accessed | tf_op | source)
XLA Modules:
  0.0 246.7 jit_solution(9349097678848998593)
XLA Ops:
  0.0 0.9 pad_maximum_fusion
  0.9 0.1 copy.9
  1.0 0.8 reshape.18.gains
  1.8 240.2 %layer_stack.1 = bf16[2,4,4,16,4096]{4,3,2,1,0:T(8,128)(2,1)} custom-call(bf16[2,4,4,16,4096]{4,3,2,1,0:T(8,128)(2,1)} %bitcast.12, bf16[3,3,4096,128]{3,2,1,0:T(8,128)(2,1)} %bitcast.11, bf16[3,128,4096]{2,1,0:T(8,128)(2,1)} %bitcast.13, bf16[3,4096,512]{2,1,0:T(8,128)(2,1)} %hu.1, bf16[3,512,4096]{2,1,0:T(8,128)(2,1)} %hd.1, f32[6,1,4096]{2,1,0:T(1,128)} %reshape.18.gains), custom_call_target="tpu_custom_call" | custom-call | tf_op jit(solution)/shard_map/layer_stack/pallas_call | solution.py:358
  242.0 4.7 %copy.11 = bf16[512,4096]{1,0:T(8,128)(2,1)} copy(bf16[512,4096]{1,0:T(8,128)(2,1)} %bitcast.10) | data formatting | bytes 8388608

commit v4 on v3

--- a/solution.py
+++ b/solution.py
@@ -20,12 +20,12 @@
     return centred * lax.rsqrt(var + 1e-5) * gain
 
 
-def stack_kernel(act, hq, ho, hu, hd, gains, out,
+def stack_kernel(act, hq, ho, hu, hd, gain1, gain2, out,
                  wq, wo, wu, wd, part, psnd, prcv, fb, gb,
                  kc, vc, ob, hid, xres,
-                 wsem, pss, psr, rss, rsr, ags, agr, dds, ddr):
+                 asem, wsem, pss, psr, rss, rsr, ags, agr, dds, ddr):
     layers = hq.shape[0]
-    rows = act.shape[1] * act.shape[2] * act.shape[3]
+    rows = SIDE * SIDE * act.shape[3]
     brow = act.shape[3]
     width = act.shape[4]
     head = hq.shape[3]
@@ -36,13 +36,14 @@
 
     t = lax.axis_index("tp")
     z = lax.axis_index("dp")
-    m = lax.rem(t, CORES)
+    core = lax.rem(t, CORES)
+    m = CORES - 1 - core
     x = lax.rem(lax.div(t, CORES), SIDE)
     y = lax.div(t, CORES * SIDE)
-    partner = t + 1 - 2 * m
+    partner = t + 1 - 2 * core
 
     def dev(yy, xx):
-        return (yy * SIDE + xx) * CORES + m
+        return (yy * SIDE + xx) * CORES + core
 
     def ring(along_x):
         me = x if along_x else y
@@ -59,32 +60,49 @@
         pl.semaphore_signal(barrier, inc=1, device_id=(z, peer), device_id_type=pl.DeviceIdType.MESH)
 
     def weight_copies(l, kind):
+        i = lax.rem(l, 2)
         if kind == 0:
             cps = [pltpu.make_async_copy(
-                hq.at[l, c], wq.at[l, :, pl.ds(c * head, head)], wsem.at[l, c]) for c in range(3)]
-            return cps + [pltpu.make_async_copy(ho.at[l], wo.at[l], wsem.at[l, 3])]
-        return [pltpu.make_async_copy(hu.at[l], wu.at[l], wsem.at[l, 4]),
-                pltpu.make_async_copy(hd.at[l], wd.at[l], wsem.at[l, 5])]
-
-    for l in range(layers):
+                hq.at[l, c], wq.at[i, :, pl.ds(c * head, head)], wsem.at[l, c]) for c in range(3)]
+            return cps + [pltpu.make_async_copy(ho.at[l], wo.at[i], wsem.at[l, 3])]
+        return [pltpu.make_async_copy(hu.at[l], wu.at[i], wsem.at[l, 4]),
+                pltpu.make_async_copy(hd.at[l], wd.at[i], wsem.at[l, 5])]
+
+    def act_copy(c, b):
+        return pltpu.make_async_copy(act.at[c, b], out.at[c, b], asem.at[c, b])
+
+    own_copy = pltpu.make_async_copy(act.at[m, y, x], xres, asem.at[CORES, 0])
+    for b in range(SIDE):
+        act_copy(0, b).start()
+    for cp in weight_copies(0, 0):
+        cp.start()
+    own_copy.start()
+    for b in range(SIDE):
+        act_copy(1, b).start()
+    for l in range(min(2, layers)):
         for kind in range(2):
-            for cp in weight_copies(l, kind):
-                cp.start()
+            if l + kind > 0:
+                for cp in weight_copies(l, kind):
+                    cp.start()
 
     kc[...] = jnp.zeros_like(kc)
     vc[...] = jnp.zeros_like(vc)
 
-    def first_norm(i, carry):
-        c = lax.div(i, SIDE)
-        b = lax.rem(i, SIDE)
-        out[c, b] = norm_rows(act[c, b].astype(F32), gains[0]).astype(BF16)
-        return carry
-
-    with jax.named_scope("first_norm"):
-        lax.fori_loop(0, CORES * SIDE, first_norm, 0)
-    xres[...] = act[m, y, x]
-
-    pl.semaphore_wait(barrier, len(peers))
+    def first_norm(c):
+        def body(b, carry):
+            act_copy(c, b).wait()
+            out[c, b] = norm_rows(out[c, b].astype(F32), gain1[pl.ds(0, 1), :]).astype(BF16)
+            return carry
+
+        with jax.named_scope("first_norm"):
+            lax.fori_loop(0, SIDE, body, 0)
+
+    first_norm(0)
+    with jax.named_scope("own_copy"):
+        own_copy.wait()
+
+    with jax.named_scope("barrier"):
+        pl.semaphore_wait(barrier, len(peers))
 
     def remote(src, dst, ss, rs, peer):
         return pltpu.make_async_remote_copy(
@@ -105,6 +123,10 @@
 
     def rs_blk(o, b1, b2, cs):
         return part.at[b2, b1, :, cs] if o == 0 else part.at[b1, b2, :, cs]
+
+    def parts(o):
+        quarter = half // 2
+        return pl.ds(o * half, quarter), pl.ds(o * half + quarter, quarter)
 
     def rs1(o, p, k):
         _, r, l, op, rdev, ldev, opdev = first[o]
@@ -156,8 +178,14 @@
         ref = ag_blk(o, first[o][0], b2_of(o, p), cols(o))
         return remote(ref, ref, ags.at[o, p, k], agr.at[o, p, k], to)
 
-    def to_partner(o, b, p):
-        ref = ag_blk(o, b, b2_of(o, p), cols(o))
+    def fwd2(o, p, k):
+        _, r, l, _, rdev, ldev, _ = first[o]
+        b, to = [(l, rdev), (r, ldev)][k]
+        ref = ag_blk(o, b, b2_of(o, p), parts(o)[k])
+        return remote(ref, ref, ags.at[o, p, 3 + k], agr.at[o, p, 3 + k], to)
+
+    def to_partner(o, b, p, cs=None):
+        ref = ag_blk(o, b, b2_of(o, p), cols(o) if cs is None else cs)
         remote(ref, ref, dds.at[0], ddr.at[0], partner).start()
 
     def whole(c):
@@ -167,8 +195,14 @@
         whole(1 - m).wait_recv()
 
     def gather_piece(o, p):
-        for k in range(3):
+        for k in (1, 2):
             ag2(o, p, k).start()
+        if p == 0:
+            ag2(o, p, 0).start()
+        else:
+            @pl.when(m == 1)
+            def _():
+                ag2(o, p, 0).start()
         to_partner(o, first[o][0], p)
 
     def p_desc(n):
@@ -176,7 +210,7 @@
 
     def attention(c, l):
         a = out[c].reshape(rows, width)
-        qkv = jnp.dot(a, wq[l], preferred_element_type=F32).astype(BF16)
+        qkv = jnp.dot(a, wq[lax.rem(l, 2)], preferred_element_type=F32).astype(BF16)
         base = pl.multiple_of(c * rows, rows)
         kc[pl.ds(base, rows), :] = qkv[:, head:2 * head]
         vc[pl.ds(base, rows), :] = qkv[:, 2 * head:]
@@ -193,7 +227,7 @@
         def body(n, carry):
             cs = pl.ds(pl.multiple_of(n * 256, 256), 256)
             a = out[c].reshape(rows, width)
-            up = jnp.dot(a, wu[l, :, cs], preferred_element_type=F32)
+            up = jnp.dot(a, wu[lax.rem(l, 2), :, cs], preferred_element_type=F32)
             hid[:, cs] = jax.nn.gelu(up, approximate=True).astype(BF16)
             return carry
         lax.fori_loop(0, hid.shape[1] // 256, body, 0)
@@ -216,7 +250,7 @@
 
         def body(n, carry, lhs, w):
             cs = pl.ds(pl.multiple_of(n * tile, tile), tile)
-            emit_tile(n, jnp.dot(lhs[...], w[l, :, cs], preferred_element_type=F32), own)
+            emit_tile(n, jnp.dot(lhs[...], w[lax.rem(l, 2), :, cs], preferred_element_type=F32), own)
             return carry
 
         @pl.when(odd == 0)
@@ -227,51 +261,84 @@
         def _():
             lax.fori_loop(lo, lo + TILES // 2, functools.partial(body, lhs=hid, w=wd), 0)
 
+    def phase1_sums(p):
+        with jax.named_scope(f"rs1_sum{p}"):
+            for o in range(2):
+                rs1_sum(o, p)
+
     def reduce_and_norm(done):
-        for p in range(SIDE):
-            with jax.named_scope(f"rs1_sum{p}"):
-                for o in range(2):
-                    rs1_sum(o, p)
         with jax.named_scope("rs2_sum"):
             for o in range(2):
                 rs2_sum(o)
         with jax.named_scope("owned_norm"):
             xs = xres[...].astype(F32)
-            gain = gains[lax.min(done + 1, halves - 1)]
+            nxt = lax.div(lax.min(done + 1, halves - 1), 2)
+            gain = jnp.where(lax.rem(done, 2) == 0, gain2[pl.ds(nxt, 1), :], gain1[pl.ds(nxt, 1), :])
             nrm = norm_rows(xs, gain)
             out[m, y, x] = jnp.where(done == halves - 1, xs, nrm).astype(BF16)
 
-    def gather_start():
+    def gather_send():
         with jax.named_scope("ag1"):
-            for k in range(3):
+            for k in (1, 2, 0):
                 for o in range(2):
                     ag1(o, k).start()
             for o in range(2):
                 gather_piece(o, 3)
+    def gather_pieces():
         for k in (1, 2, 0):
             with jax.named_scope(f"ag1_{k}"):
                 for o in range(2):
                     ag1(o, k).wait_recv()
                     gather_piece(o, (0, 2, 1)[k])
 
-    def gather_end():
-        for p in (3, 2, 1, 0):
-            with jax.named_scope(f"ag2_{p}"):
-                for o in range(2):
-                    for k in range(3):
-                        ag2(o, p, k).wait_recv()
-                        to_partner(o, first[o][(3, 2, 1)[k]], p)
+    def gather_end(p, ks=(1, 2, 0)):
+        with jax.named_scope(f"ag2_{p}"):
+            for o in range(2):
+                for k in ks:
+                    ag2(o, p, k).wait_recv()
+                    to_partner(o, first[o][(3, 2, 1)[k]], p)
+
+    def gather_forward(p):
+        with jax.named_scope(f"ag2_{p}"):
+            for o in range(2):
+                for k in range(2):
+                    ag2(o, p, 1 + k).wait_recv()
+                    fwd2(o, p, k).start()
+                    to_partner(o, first[o][2 - k], p)
+
+    def gather_forwarded(p):
+        with jax.named_scope(f"ag2_{p}_forwarded"):
+            for o in range(2):
+                for k in range(2):
+                    fwd2(o, p, k).wait_recv()
+                    to_partner(o, first[o][3], p, parts(o)[k])
 
     def drain():
         with jax.named_scope("drain"):
             for o in range(2):
+                for p in range(SIDE):
+                    for k in range(3):
+                        rs1(o, p, k).wait_send()
+                    if p > 0:
+                        @pl.when(m == 0)
+                        def _():
+                            for k in range(2):
+                                fwd2(o, p, k).wait_send()
+
+                        @pl.when(m == 1)
+                        def _():
+                            ag2(o, p, 0).wait_send()
+
+                    for k in range(3) if p == 0 else (1, 2):
+                        ag2(o, p, k).wait_send()
                 for k in range(3):
-                    for p in range(SIDE):
-                        rs1(o, p, k).wait_send()
-                        ag2(o, p, k).wait_send()
                     rs2(o, k).wait_send()
                     ag1(o, k).wait_send()
             whole(m).wait_send()
+
+    def wait_shares():
+        for n in range(TILES):
+            p_desc(n).wait_send()
 
     def slot(s, carry):
         c = lax.rem(s, CORES)
@@ -281,8 +348,21 @@
         own = c == m
         other = c != m
         inside = s < slots
-
-        @pl.when(jnp.logical_and(other, s >= CORES))
+        late = jnp.logical_and(jnp.logical_and(c == 0, other), s >= 1)
+
+        @pl.when(s == 1)
+        def _():
+            first_norm(1)
+
+        coming = lax.div(s, 2 * CORES) + 1
+
+        @pl.when(jnp.logical_and(lax.rem(s, 2 * CORES) == 0, jnp.logical_and(coming >= 2, coming < layers)))
+        def _():
+            for kind in range(2):
+                for cp in weight_copies(coming, kind):
+                    cp.start()
+
+        @pl.when(jnp.logical_and(jnp.logical_and(inside, other), s >= CORES))
         def _():
             with jax.named_scope("wait_other"):
                 wait_other()
@@ -292,15 +372,24 @@
             def _():
                 @pl.when(c == 0)
                 def _():
-                    for cp in weight_copies(l, kind):
-                        cp.wait()
+                    with jax.named_scope("weights"):
+                        for cp in weight_copies(l, kind):
+                            cp.wait()
 
                 with jax.named_scope("up"):
                     (attention, mlp_up)[kind](c, l)
 
+        @pl.when(late)
+        def _():
+            gather_end(3)
+
         @pl.when(jnp.logical_and(jnp.logical_and(inside, own), s >= CORES))
         def _():
             drain()
+
+        @pl.when(jnp.logical_and(jnp.logical_and(inside, other), s >= CORES))
+        def _():
+            wait_shares()
 
         for o in range(2):
             @pl.when(inside)
@@ -312,28 +401,45 @@
             def _():
                 rs1_start(o)
 
+            @pl.when(late)
+            def _():
+                for p in ((2,), (1, 0))[o]:
+                    gather_end(p)
+
+            if o == 0:
+                @pl.when(jnp.logical_and(c == 1, other))
+                def _():
+                    phase1_sums(0)
+
+        @pl.when(jnp.logical_and(c == 1, own))
+        def _():
+            phase1_sums(0)
+
         @pl.when(c == 1)
         def _():
+            for p in range(1, SIDE):
+                phase1_sums(p)
             reduce_and_norm(h)
-            gather_start()
-
-        @pl.when(jnp.logical_and(s >= 1, other))
-        def _():
-            gather_end()
-
-        @pl.when(jnp.logical_and(inside, other))
-        def _():
-            for n in range(TILES):
-                p_desc(n).wait_send()
+            gather_send()
+            gather_pieces()
+
+        @pl.when(jnp.logical_and(c == 1, other))
+        def _():
+            gather_forward(3)
+            gather_forward(2)
+            gather_forward(1)
+            gather_forwarded(3)
+            gather_end(0)
+            gather_forwarded(2)
+            gather_forwarded(1)
 
         return carry
 
     lax.fori_loop(0, slots + 1, slot, 0)
     drain()
-
-    @pl.when(m == 0)
-    def _():
-        wait_other()
+    wait_shares()
+
+    wait_other()
 
 
 def solution(mesh):
@@ -348,23 +454,22 @@
         assert tp == SIDE * SIDE * CORES
         blocks = (CORES, SIDE, SIDE, brow, width)
         q_view = jnp.transpose(w_qkv, (0, 2, 3, 1, 4)).reshape(layers, 3, width, head)
-        gains = jnp.stack([gain_one, gain_two], axis=1).reshape(2 * layers, 1, width)
         half = width // 2
         tile = width // TILES
         vmem = pltpu.VMEM
         dma = pltpu.SemaphoreType.DMA
-        any_spec = pl.BlockSpec(memory_space=pl.ANY)
+        hbm_spec = pl.BlockSpec(memory_space=pltpu.HBM)
         vmem_spec = pl.BlockSpec(memory_space=pltpu.VMEM)
         res = pl.pallas_call(
             stack_kernel,
             out_shape=jax.ShapeDtypeStruct(blocks, BF16),
-            in_specs=[vmem_spec, any_spec, any_spec, any_spec, any_spec, vmem_spec],
+            in_specs=[hbm_spec] * 5 + [vmem_spec] * 2,
             out_specs=vmem_spec,
             scratch_shapes=[
-                vmem((layers, width, 3 * head), BF16),
-                vmem((layers, head, width), BF16),
-                vmem((layers, width, ffn), BF16),
-                vmem((layers, ffn, width), BF16),
+                vmem((2, width, 3 * head), BF16),
+                vmem((2, head, width), BF16),
+                vmem((2, width, ffn), BF16),
+                vmem((2, ffn, width), BF16),
                 vmem((SIDE, SIDE, brow, width), BF16),
                 vmem((TILES, rows, tile), BF16),
                 vmem((TILES, rows, tile), BF16),
@@ -373,16 +478,16 @@
                 vmem((seq, head), BF16), vmem((seq, head), BF16),
                 vmem((rows, head), BF16), vmem((rows, ffn), BF16),
                 vmem((brow, width), BF16),
-                dma((layers, 6)),
+                dma((CORES + 1, SIDE)), dma((layers, 6)),
                 dma((TILES,)), dma((TILES,)),
                 dma((2, SIDE + 1, 3)), dma((2, SIDE + 1, 3)),
-                dma((2, SIDE + 1, 3)), dma((2, SIDE + 1, 3)),
+                dma((2, SIDE + 1, 5)), dma((2, SIDE + 1, 5)),
                 dma((1,)), dma((1,)),
             ],
             compiler_params=pltpu.CompilerParams(
-                collective_id=0, has_side_effects=True, vmem_limit_bytes=63 * 2 ** 20),
+                collective_id=0, has_side_effects=True, vmem_limit_bytes=46 * 2 ** 20),
             name="layer_stack",
-        )(act_in.reshape(blocks), q_view, w_out.reshape(layers, head, width), w_up, w_down, gains)
+        )(act_in.reshape(blocks), q_view, w_out.reshape(layers, head, width), w_up, w_down, gain_one, gain_two)
         return res.reshape(seq, width)
 
     return jax.shard_map(

time: 247 us -> 227 us (0.919)
  Pallas kernels: 240 us -> 222 us
    pallas_call x1, Pallas kernels: 240 us -> 222 us  [device_fn(): pl.pallas_call(stack_kernel, out_shape=jax.ShapeDtypeStruct(blocks, BF16)...]
    unnamed x1 -> x7, local copies, waits for them, and re-layouts: 4.7 us -> 5.58 us
where the time goes in v4:
time: 227 us
  Pallas kernels  222 us (98%)
  local copies, waits for them, and re-layouts  5.58 us (2%)
    pallas_call x1, Pallas kernels, device_fn(): pl.pallas_call(stack_kernel, out_shape=jax.ShapeDtypeStruct(blocks, BF16)...  222 us
    unnamed x7, local copies, waits for them, and re-layouts  5.58 us

profile of v4, /device:TPU:97, one launch (start us, length us, event | category | flops | bytes accessed | tf_op | source)
XLA Modules:
  0.0 227.2 jit_solution(8678537082014156361)
XLA Ops:
  0.0 0.0 copy-start
  0.0 1.9 copy-done
  1.9 0.0 copy-start.1
  1.9 0.8 copy-done.1
  2.7 0.0 copy-start.2
  2.7 0.8 copy-done.2
  3.6 221.6 %layer_stack.1 = bf16[2,4,4,16,4096]{4,3,2,1,0:T(8,128)(2,1)S(1)} custom-call(bf16[2,4,4,16,4096]{4,3,2,1,0:T(8,128)(2,1)} %bitcast.11, bf16[3,3,4096,128]{3,2,1,0:T(8,128)(2,1)} %bitcast.10, bf16[3,128,4096]{2,1,0:T(8,128)(2,1)S(1)} %bitcast.9, bf16[3,4096,512]{2,1,0:T(8,128)(2,1)} %hu.1, bf16[3,512,4096]{2,1,0:T(8,128)(2,1)} %hd.1, ...), custom_call_target="tpu_custom_call" | custom-call | tf_op jit(solution)/shard_map/layer_stack/pallas_call | solution.py:463
  225.1 2.0 copy.10
Async XLA Ops:
  0.0 1.9 copy-start
  1.9 0.8 copy-start.1
  2.7 0.8 copy-start.2

commit v5 on v4

--- a/solution.py
+++ b/solution.py
@@ -11,6 +11,7 @@
 BF16 = jnp.bfloat16
 SIDE = 4
 CORES = 2
+EARLY = (0, 1)
 TILES = 8
 
 
@@ -98,8 +99,6 @@
             lax.fori_loop(0, SIDE, body, 0)
 
     first_norm(0)
-    with jax.named_scope("own_copy"):
-        own_copy.wait()
 
     with jax.named_scope("barrier"):
         pl.semaphore_wait(barrier, len(peers))
@@ -124,15 +123,22 @@
     def rs_blk(o, b1, b2, cs):
         return part.at[b2, b1, :, cs] if o == 0 else part.at[b1, b2, :, cs]
 
+    def rs1(o, p, k, i=None):
+        _, r, l, op, rdev, ldev, opdev = first[o]
+        b, to = [(op, opdev), (r, rdev), (l, ldev)][k]
+        if i is None:
+            src, dst, j = rs_blk(o, b, b2_of(o, p), cols(o)), fb.at[o, k, p], k
+        else:
+            src, dst, j = rs_blk(o, b, b2_of(o, p), parts(o)[i]), fb.at[o, k, p, :, parts(0)[i]], 3 * i + k
+        return remote(src, dst, rss.at[o, p, j], rsr.at[o, p, j], to)
+
+    def rs1_all(o, p):
+        halves_of = (0, 1) if p in EARLY else (None,)
+        return [rs1(o, p, k, i) for i in halves_of for k in range(3)]
+
     def parts(o):
         quarter = half // 2
         return pl.ds(o * half, quarter), pl.ds(o * half + quarter, quarter)
-
-    def rs1(o, p, k):
-        _, r, l, op, rdev, ldev, opdev = first[o]
-        b, to = [(op, opdev), (r, rdev), (l, ldev)][k]
-        src = rs_blk(o, b, b2_of(o, p), cols(o))
-        return remote(src, fb.at[o, k, p], rss.at[o, p, k], rsr.at[o, p, k], to)
 
     def rs2(o, k):
         _, r, l, op, rdev, ldev, opdev = second[o]
@@ -145,14 +151,19 @@
             total = total + other[...].astype(F32)
         return total
 
-    def rs1_start(o):
-        for p in range(SIDE):
+    def rs1_start(o, i):
+        for p in EARLY:
             for k in range(3):
-                rs1(o, p, k).start()
+                rs1(o, p, k, i).start()
+        if i == 1:
+            for p in range(SIDE):
+                if p not in EARLY:
+                    for cp in rs1_all(o, p):
+                        cp.start()
 
     def rs1_sum(o, p):
-        for k in range(3):
-            rs1(o, p, k).wait_recv()
+        for cp in rs1_all(o, p):
+            cp.wait_recv()
         blk = rs_blk(o, first[o][0], b2_of(o, p), cols(o))
         blk[...] = add_to(blk, *(fb.at[o, k, p] for k in range(3))).astype(BF16)
         if p < 3:
@@ -245,8 +256,8 @@
             psnd[n] = acc.astype(BF16)
             p_desc(n).start()
 
-    def down(o, l, odd, own):
-        lo = o * (TILES // 2)
+    def down(o, i, l, odd, own):
+        lo = (2 * o + i) * (TILES // 4)
 
         def body(n, carry, lhs, w):
             cs = pl.ds(pl.multiple_of(n * tile, tile), tile)
@@ -255,11 +266,11 @@
 
         @pl.when(odd == 0)
         def _():
-            lax.fori_loop(lo, lo + TILES // 2, functools.partial(body, lhs=ob, w=wo), 0)
+            lax.fori_loop(lo, lo + TILES // 4, functools.partial(body, lhs=ob, w=wo), 0)
 
         @pl.when(odd == 1)
         def _():
-            lax.fori_loop(lo, lo + TILES // 2, functools.partial(body, lhs=hid, w=wd), 0)
+            lax.fori_loop(lo, lo + TILES // 4, functools.partial(body, lhs=hid, w=wd), 0)
 
     def phase1_sums(p):
         with jax.named_scope(f"rs1_sum{p}"):
@@ -317,8 +328,8 @@
         with jax.named_scope("drain"):
             for o in range(2):
                 for p in range(SIDE):
-                    for k in range(3):
-                        rs1(o, p, k).wait_send()
+                    for cp in rs1_all(o, p):
+                        cp.wait_send()
                     if p > 0:
                         @pl.when(m == 0)
                         def _():
@@ -353,6 +364,7 @@
         @pl.when(s == 1)
         def _():
             first_norm(1)
+            own_copy.wait()
 
         coming = lax.div(s, 2 * CORES) + 1
 
@@ -391,22 +403,25 @@
         def _():
             wait_shares()
 
-        for o in range(2):
+        for q in range(4):
+            o, i = q % 2, q // 2
+
             @pl.when(inside)
             def _():
                 with jax.named_scope("down"):
-                    down(o, l, odd, own)
+                    down(o, i, l, odd, own)
 
             @pl.when(jnp.logical_and(inside, own))
             def _():
-                rs1_start(o)
-
-            @pl.when(late)
-            def _():
-                for p in ((2,), (1, 0))[o]:
-                    gather_end(p)
-
-            if o == 0:
+                rs1_start(o, i)
+
+            if q in (1, 3):
+                @pl.when(late)
+                def _():
+                    for p in {1: (2,), 3: (1, 0)}[q]:
+                        gather_end(p)
+
+            if q == 1:
                 @pl.when(jnp.logical_and(c == 1, other))
                 def _():
                     phase1_sums(0)
@@ -480,7 +495,7 @@
                 vmem((brow, width), BF16),
                 dma((CORES + 1, SIDE)), dma((layers, 6)),
                 dma((TILES,)), dma((TILES,)),
-                dma((2, SIDE + 1, 3)), dma((2, SIDE + 1, 3)),
+                dma((2, SIDE + 1, 6)), dma((2, SIDE + 1, 6)),
                 dma((2, SIDE + 1, 5)), dma((2, SIDE + 1, 5)),
                 dma((1,)), dma((1,)),
             ],

time: 227 us -> 219 us (0.965)
  Pallas kernels: 222 us -> 213 us
    pallas_call x1, Pallas kernels: 222 us -> 213 us  [device_fn(): pl.pallas_call(stack_kernel, out_shape=jax.ShapeDtypeStruct(blocks, BF16)...]
where the time goes in v5:
time: 219 us
  Pallas kernels  213 us (97%)
  local copies, waits for them, and re-layouts  5.58 us (3%)
    pallas_call x1, Pallas kernels, device_fn(): pl.pallas_call(stack_kernel, out_shape=jax.ShapeDtypeStruct(blocks, BF16)...  213 us
    unnamed x7, local copies, waits for them, and re-layouts  5.58 us

profile of v5, /device:TPU:97, one launch (start us, length us, event | category | flops | bytes accessed | tf_op | source)
XLA Modules:
  0.0 219.0 jit_solution(16663045454460056162)
XLA Ops:
  0.0 0.0 copy-start
  0.0 1.9 copy-done
  1.9 0.0 copy-start.1
  1.9 0.8 copy-done.1
  2.7 0.0 copy-start.2
  2.7 0.8 copy-done.2
  3.6 213.4 %layer_stack.1 = bf16[2,4,4,16,4096]{4,3,2,1,0:T(8,128)(2,1)S(1)} custom-call(bf16[2,4,4,16,4096]{4,3,2,1,0:T(8,128)(2,1)} %bitcast.11, bf16[3,3,4096,128]{3,2,1,0:T(8,128)(2,1)} %bitcast.10, bf16[3,128,4096]{2,1,0:T(8,128)(2,1)S(1)} %bitcast.9, bf16[3,4096,512]{2,1,0:T(8,128)(2,1)} %hu.1, bf16[3,512,4096]{2,1,0:T(8,128)(2,1)} %hd.1, ...), custom_call_target="tpu_custom_call" | custom-call | tf_op jit(solution)/shard_map/layer_stack/pallas_call | solution.py:478
  216.9 2.0 copy.10
Async XLA Ops:
  0.0 1.9 copy-start
  1.9 0.8 copy-start.1
  2.7 0.8 copy-start.2

commit v6 on v5

--- a/solution.py
+++ b/solution.py
@@ -21,9 +21,9 @@
     return centred * lax.rsqrt(var + 1e-5) * gain
 
 
-def stack_kernel(act, hq, ho, hu, hd, gain1, gain2, out,
+def stack_kernel(act, hq, ho, hu, hd, hg1, hg2, out,
                  wq, wo, wu, wd, part, psnd, prcv, fb, gb,
-                 kc, vc, ob, hid, xres,
+                 kc, vc, ob, hid, xres, gain1, gain2,
                  asem, wsem, pss, psr, rss, rsr, ags, agr, dds, ddr):
     layers = hq.shape[0]
     rows = SIDE * SIDE * act.shape[3]
@@ -72,7 +72,11 @@
     def act_copy(c, b):
         return pltpu.make_async_copy(act.at[c, b], out.at[c, b], asem.at[c, b])
 
+    gain_copies = [pltpu.make_async_copy(hg1, gain1, asem.at[CORES, 1]),
+                   pltpu.make_async_copy(hg2, gain2, asem.at[CORES, 2])]
     own_copy = pltpu.make_async_copy(act.at[m, y, x], xres, asem.at[CORES, 0])
+    for cp in gain_copies:
+        cp.start()
     for b in range(SIDE):
         act_copy(0, b).start()
     for cp in weight_copies(0, 0):
@@ -98,6 +102,8 @@
         with jax.named_scope("first_norm"):
             lax.fori_loop(0, SIDE, body, 0)
 
+    for cp in gain_copies:
+        cp.wait()
     first_norm(0)
 
     with jax.named_scope("barrier"):
@@ -421,10 +427,10 @@
                     for p in {1: (2,), 3: (1, 0)}[q]:
                         gather_end(p)
 
-            if q == 1:
+            if q in (1, 2):
                 @pl.when(jnp.logical_and(c == 1, other))
                 def _():
-                    phase1_sums(0)
+                    phase1_sums(q - 1)
 
         @pl.when(jnp.logical_and(c == 1, own))
         def _():
@@ -432,7 +438,11 @@
 
         @pl.when(c == 1)
         def _():
-            for p in range(1, SIDE):
+            @pl.when(own)
+            def _():
+                phase1_sums(1)
+
+            for p in range(2, SIDE):
                 phase1_sums(p)
             reduce_and_norm(h)
             gather_send()
@@ -475,10 +485,13 @@
         dma = pltpu.SemaphoreType.DMA
         hbm_spec = pl.BlockSpec(memory_space=pltpu.HBM)
         vmem_spec = pl.BlockSpec(memory_space=pltpu.VMEM)
+        def pin(array):
+            return pltpu.with_memory_space_constraint(array, pltpu.HBM)
+
         res = pl.pallas_call(
             stack_kernel,
             out_shape=jax.ShapeDtypeStruct(blocks, BF16),
-            in_specs=[hbm_spec] * 5 + [vmem_spec] * 2,
+            in_specs=[hbm_spec] * 7,
             out_specs=vmem_spec,
             scratch_shapes=[
                 vmem((2, width, 3 * head), BF16),
@@ -493,6 +506,7 @@
                 vmem((seq, head), BF16), vmem((seq, head), BF16),
                 vmem((rows, head), BF16), vmem((rows, ffn), BF16),
                 vmem((brow, width), BF16),
+                vmem((layers, width), F32), vmem((layers, width), F32),
                 dma((CORES + 1, SIDE)), dma((layers, 6)),
                 dma((TILES,)), dma((TILES,)),
                 dma((2, SIDE + 1, 6)), dma((2, SIDE + 1, 6)),
@@ -502,7 +516,8 @@
             compiler_params=pltpu.CompilerParams(
                 collective_id=0, has_side_effects=True, vmem_limit_bytes=46 * 2 ** 20),
             name="layer_stack",
-        )(act_in.reshape(blocks), q_view, w_out.reshape(layers, head, width), w_up, w_down, gain_one, gain_two)
+        )(act_in.reshape(blocks), q_view, pin(w_out.reshape(layers, head, width)), w_up, w_down,
+          pin(gain_one), pin(gain_two))
         return res.reshape(seq, width)
 
     return jax.shard_map(

time: 219 us -> 217 us (level)
  local copies, waits for them, and re-layouts: 5.58 us -> 2.02 us
    unnamed x7 -> x1, local copies, waits for them, and re-layouts: 5.58 us -> 2.02 us
where the time goes in v6:
time: 217 us
  Pallas kernels  215 us (99%)
    pallas_call x1, Pallas kernels, device_fn(): pl.pallas_call(stack_kernel, out_shape=jax.ShapeDtypeStruct(blocks, BF16)...  215 us

profile of v6, /device:TPU:97, one launch (start us, length us, event | category | flops | bytes accessed | tf_op | source)
XLA Modules:
  0.0 217.2 jit_solution(10832396747217454654)
XLA Ops:
  0.0 215.2 %layer_stack.1 = bf16[2,4,4,16,4096]{4,3,2,1,0:T(8,128)(2,1)S(1)} custom-call(bf16[2,4,4,16,4096]{4,3,2,1,0:T(8,128)(2,1)} %bitcast.10, bf16[3,3,4096,128]{3,2,1,0:T(8,128)(2,1)} %bitcast.9, bf16[3,128,4096]{2,1,0:T(8,128)(2,1)} %bitcast.11, bf16[3,4096,512]{2,1,0:T(8,128)(2,1)} %hu.1, bf16[3,512,4096]{2,1,0:T(8,128)(2,1)} %hd.1, f32[3,4096]{1,0:T(4,128)} %hg1.1, ...), custom_call_target="tpu_custom_call" | custom-call | tf_op jit(solution)/shard_map/layer_stack/pallas_call | solution.py:491
  215.2 2.0 copy.10
